TPU v7x, 128 devices: a whole 4x4x4 slice. The times are simulated.
128 devices in a mesh: fsdp: 16 (over x_lo, y, core), expert: 8 (over x_hi, z).
Axes of the slice: x: 4 (x_hi: 2, x_lo: 2; x = x_hi * 2 + x_lo), y: 4, z: 4, core: 2. Of those that a mesh axis runs over, the one named last changes fastest.
Arguments:
- pool: bfloat16 [256, 128, 4096], P('fsdp', None, 'expert'), may hold values from -6 to 6
- picks: int32 [16, 8], P('fsdp'), may hold values from 0 to 15, as said below
- lengths: int32 [256], P('fsdp'), may hold values from 1 to 128
- routes: int32 [16384, 2], P(('fsdp', 'expert')), may hold values from 0 to 7, all different within a row; in each aligned block of 128 rows (0 to 127, 128 to 255, ...) at most 64 rows name the same one
- route_gap: float32 [16384], P(('fsdp', 'expert')), may hold values from -8 to 8
- gate_weight: bfloat16 [8, 14336, 4096], P('expert', 'fsdp'), may hold values from -0.09375 to 0.09375
- down_weight: bfloat16 [8, 14336, 4096], P('expert', 'fsdp'), may hold values from -0.046875 to 0.046875
Outputs:
- moe_out: bfloat16 [16384, 4096], P(('fsdp', 'expert'))
Inputs may be any that keep to these rules, and one draw needn't show every extreme that they name: `picks`: each row holds 8 different candidate numbers. `routes`: the two experts of a token differ; among the 128 tokens of one window no expert is named by more than 64 tokens.
All inputs are finite; a program needn't handle non-finite values.
Results may differ from a plain program's by a relative error of at most 0.019.
Values may be sent and summed in bfloat16 or wider, within the bound.
A program may use at most 128 MiB of HBM per device.

v0:
```python
import jax
import jax.numpy as jnp
from jax import lax
from jax.sharding import PartitionSpec as P

EXPERTS = 8
TOP = 2
CAP = 14


def sent_to_all(value, axis):
    length = lax.axis_size(axis)
    return lax.all_to_all(
        jnp.broadcast_to(value[None], (length, *value.shape)), axis, 0, 0, tiled=True
    )


def laid_out(tiles, dim):
    shape = list(tiles.shape[1:])
    shape[dim] *= tiles.shape[0]
    return jnp.moveaxis(tiles, 0, dim).reshape(shape)


def collect(value, axis, dim):
    tiles = sent_to_all(value, axis)
    return laid_out(tiles, dim)


def slot_targets(block_routes, length):
    row_count = block_routes.shape[0]
    is_live = jnp.arange(row_count, dtype=jnp.int32) < length
    expert_ids = jnp.concatenate([block_routes[:, 0], block_routes[:, 1]])
    live_both = jnp.concatenate([is_live, is_live])
    expert_hits = (
        (expert_ids[:, None] == jnp.arange(EXPERTS, dtype=jnp.int32)[None, :]) & live_both[:, None]
    ).astype(jnp.int32)
    earlier = jnp.cumsum(expert_hits, axis=0) - expert_hits
    slot_rank = jnp.sum(earlier * expert_hits, axis=1)
    is_kept = live_both & (slot_rank < CAP)
    return jnp.where(is_kept, expert_ids * CAP + slot_rank, -1)


def dispatch_table(targets):
    row_count = targets.shape[0] // 2
    slot_ids = jnp.arange(EXPERTS * CAP, dtype=jnp.int32)[:, None]
    return (
        (slot_ids == targets[None, :row_count]) | (slot_ids == targets[None, row_count:])
    ).astype(jnp.bfloat16)


def combine_table(targets, gap_row):
    row_count = targets.shape[0] // 2
    slot_ids = jnp.arange(EXPERTS * CAP, dtype=jnp.int32)[None, :]
    weight_first = jax.nn.sigmoid(gap_row)[:, None]
    weight_second = jax.nn.sigmoid(-gap_row)[:, None]
    first_hit = (targets[:row_count, None] == slot_ids).astype(jnp.float32)
    second_hit = (targets[row_count:, None] == slot_ids).astype(jnp.float32)
    return first_hit * weight_first + second_hit * weight_second


def local(pool, picks, lengths, routes, route_gap, gate_weight, down_weight):
    expert_count = lax.axis_size("expert")
    expert_local = gate_weight.shape[0]
    window_rows = pool.shape[1]
    model_width = gate_weight.shape[2]
    my_column = lax.axis_index("expert")
    chosen = picks[0]
    selected = jnp.take(pool, chosen, axis=0)
    chosen_len = jnp.take(lengths, chosen)
    column_routes = collect(routes, "expert", 0)
    all_targets = jax.vmap(slot_targets)(
        column_routes.reshape(expert_count, window_rows, TOP), chosen_len
    )
    tables = jax.vmap(dispatch_table)(all_targets)
    outgoing = jnp.einsum(
        "bsp,bpd->bsd", tables, selected, preferred_element_type=jnp.float32
    ).astype(jnp.bfloat16)
    outgoing = outgoing.reshape(expert_count, expert_count, expert_local, CAP, selected.shape[2])
    arrived = lax.all_to_all(outgoing, "expert", split_axis=1, concat_axis=4, tiled=True)
    arrived = arrived.reshape(expert_count, expert_local, CAP, model_width)
    my_targets = lax.dynamic_index_in_dim(all_targets, my_column, 0, keepdims=False)
    gate_act = jnp.einsum(
        "fbecd,ehd->fbech",
        lax.all_gather(arrived[None], "fsdp", axis=0, tiled=True),
        gate_weight,
        preferred_element_type=jnp.float32,
    )
    hidden = jax.nn.silu(gate_act).astype(jnp.bfloat16)
    dev_rows = expert_count * expert_local * CAP
    partial_value = jnp.einsum(
        "fbech,ehd->fbecd", hidden, down_weight, preferred_element_type=jnp.float32
    )
    summed = lax.psum_scatter(
        partial_value.reshape(dev_rows * lax.axis_size("fsdp"), model_width).astype(jnp.bfloat16),
        "fsdp",
        scatter_dimension=0,
        tiled=True,
    )
    expert_out = summed.reshape(expert_count, expert_local, CAP, model_width)
    returned = lax.all_to_all(expert_out, "expert", split_axis=0, concat_axis=1, tiled=True)
    flat_out = returned.reshape(EXPERTS * CAP, model_width).astype(jnp.float32)
    combine = combine_table(my_targets, route_gap)
    mixed = jnp.dot(combine, flat_out, preferred_element_type=jnp.float32)
    return mixed.astype(jnp.bfloat16)


def solution(mesh):
    placed = (
        P("fsdp", None, "expert"),
        P("fsdp", None),
        P("fsdp"),
        P(("fsdp", "expert"), None),
        P(("fsdp", "expert")),
        P("expert", "fsdp", None),
        P("expert", "fsdp", None),
    )
    return jax.shard_map(
        local, mesh=mesh, in_specs=placed, out_specs=P(("fsdp", "expert"), None), check_vma=False
    )
```

profile of v0, /device:TPU:0, one launch (start us, length us, event | category | flops | bytes accessed | tf_op | source)
XLA Modules:
  0.0 329.3 jit_solution(543143658603108437)
XLA Ops:
  6.5 0.0 copy-start
  6.5 1.4 broadcast_in_dim.17
  8.0 7.9 %all-to-all-start = ((s32[8,128,2]{1,2,0:T(2,128)}), s32[8,128,2]{1,2,0:T(2,128)S(1)}, u32[]{:S(2)}, u32[]{:S(2)}) async-start(s32[8,128,2]{1,2,0:T(2,128)} %broadcast_in_dim.17), calls=%async_computation | async-start | bytes 16384 | tf_op jit(solution)/shard_map/all_to_all | solution.py:13
  15.9 0.0 all-gather.2.cloned.1.call-start
  15.9 0.7 fusion.35
  16.6 1.3 gather_fusion
  17.9 0.7 broadcast_select_fusion
  18.5 0.1 iota_compare_fusion.10
  18.6 0.1 iota_compare_fusion.9
  18.7 0.0 copy-done
  18.7 0.6 gather_fusion.1
  19.3 4.2 %all-to-all-done = s32[8,128,2]{1,2,0:T(2,128)S(1)} async-done(((s32[8,128,2]{1,2,0:T(2,128)}), s32[8,128,2]{1,2,0:T(2,128)S(1)}, u32[]{:S(2)}, u32[]{:S(2)}) %all-to-all-start) | async-done | bytes 8224 | tf_op jit(solution)/shard_map/all_to_all | solution.py:13
  23.6 4.5 %reduce-window.6 = s32[8,8,2,128]{3,1,2,0:T(8,128)S(1)} reduce-window(s32[8,8,2,128]{3,1,2,0:T(8,128)S(1)} %fusion.27, s32[]{:T(128)} %constant.36.clone.1), window={size=1x1x1x128 pad=0_0x0_0x0_0x127_0}, to_apply=%region_0.1 | reduce-window | flops 2080768 | bytes 131076 | tf_op jit(solution)/shard_map/reduce-window
  28.1 0.1 slice.40
  28.2 0.2 copy.28
  28.4 0.1 fusion.33
  28.5 0.1 fusion.21
  28.6 0.5 convolution_convert_fusion.1
  29.1 0.5 copy.30
  29.6 18.0 %all_to_all.29 = bf16[8,8,1,14,512]{4,0,3,2,1:T(8,128)(2,1)S(1)} all-to-all(bf16[8,8,1,14,512]{4,0,3,2,1:T(8,128)(2,1)S(1)} %bitcast.91), channel_id=1, replica_groups=mesh['fsdp'=16,'expert'=8] {'expert'}, dimensions={1} | all-to-all | bytes 1835008 | tf_op jit(solution)/shard_map/all_to_all | solution.py:79
  47.6 0.5 copy.32
  48.1 1.3 broadcast_in_dim_reshape.3
  49.5 0.0 all-gather.2.cloned.1.call-update
  49.5 0.2 reduce-scatter.2.cloned.1.call-start
  49.7 78.9 %all-gather.2.cloned.1.call-done = bf16[16,8,1,14,4096]{4,1,3,2,0:T(8,128)(2,1)} async-done(((bf16[1,8,1,14,4096]{4,1,3,2,0:T(8,128)(2,1)}), bf16[16,8,1,14,4096]{4,1,3,2,0:T(8,128)(2,1)}) %all-gather.2.cloned.1.call-update) | async-done | bytes 14680080 | tf_op jit(solution)/shard_map/all_gather | solution.py:84
  128.6 20.7 %fusion.7 = bf16[16,8,1,14,896]{4,1,3,0,2:T(8,128)(2,1)S(1)} fusion(bf16[1,896,4096]{2,1,0:T(8,128)(2,1)} %param.12, bf16[16,8,1,14,4096]{4,1,3,2,0:T(8,128)(2,1)} %all-gather.2.cloned.1.call-done), kind=kOutput, calls=%fused_computation.12 | convolution fusion | flops 13161365504 | bytes 25231360 | tf_op jit(solution)/shard_map/fbecd,ehd->fbech/dot_general | solution.py:82
  149.4 20.9 %convert_bitcast_fusion = bf16[16,8,1,14,4096]{4,1,3,0,2:T(8,128)(2,1)} fusion(bf16[1,896,4096]{2,1,0:T(8,128)(2,1)} %param.13, bf16[16,8,1,14,896]{4,1,3,0,2:T(8,128)(2,1)S(1)} %fusion.7), kind=kOutput, calls=%fused_computation.4 | convolution fusion | flops 13160677376 | bytes 25231360 | tf_op jit(solution)/shard_map/fbech,ehd->fbecd/dot_general | solution.py:90
  170.3 17.5 %copy.33 = bf16[16,8,1,14,4096]{4,3,1,0,2:T(8,128)(2,1)} copy(bf16[16,8,1,14,4096]{4,1,3,0,2:T(8,128)(2,1)} %convert_bitcast_fusion) | data formatting | bytes 29360128 | tf_op jit(solution)/shard_map/convert_element_type | solution.py:94
  187.7 18.0 %convert_element_type.43 = bf16[1792,4096]{1,0:T(8,128)(2,1)} reshape(bf16[16,8,1,14,4096]{4,3,1,0,2:T(8,128)(2,1)} %copy.33) | data formatting | bytes 29360128 | tf_op jit(solution)/shard_map/convert_element_type | solution.py:94
  205.8 0.0 copy-start.2
  205.8 0.0 reduce-scatter.2.cloned.1.call-update
  205.8 0.0 copy-start.1
  205.8 90.1 %reduce-scatter.2.cloned.1.call-done = bf16[112,4096]{1,0:T(8,128)(2,1)} async-done(((bf16[1792,4096]{1,0:T(8,128)(2,1)}), bf16[112,4096]{1,0:T(8,128)(2,1)}) %reduce-scatter.2.cloned.1.call-update) | async-done | bytes 917520 | tf_op jit(solution)/shard_map/reduce_scatter | solution.py:93
  295.9 2.4 reshape.152
  298.3 6.8 %all-to-all-start.2 = ((bf16[8,1,14,4096]{3,2,1,0:T(8,128)(2,1)}), bf16[8,1,14,4096]{3,2,1,0:T(8,128)(2,1)S(1)}, u32[]{:S(2)}, u32[]{:S(2)}) async-start(bf16[8,1,14,4096]{3,2,1,0:T(8,128)(2,1)} %bitcast.90), calls=%async_computation.3 | async-start | bytes 2097152 | tf_op jit(solution)/shard_map/all_to_all | solution.py:100
  305.1 0.0 copy-done.2
  305.1 0.1 dynamic-slice_bitcast_fusion.1
  305.2 13.4 %all-to-all-done.2 = bf16[8,1,14,4096]{3,2,1,0:T(8,128)(2,1)S(1)} async-done(((bf16[8,1,14,4096]{3,2,1,0:T(8,128)(2,1)}), bf16[8,1,14,4096]{3,2,1,0:T(8,128)(2,1)S(1)}, u32[]{:S(2)}, u32[]{:S(2)}) %all-to-all-start.2) | async-done | bytes 917536 | tf_op jit(solution)/shard_map/all_to_all | solution.py:100
  318.6 1.2 reshape.153
  319.8 2.7 convolution_convert_fusion
  322.4 0.0 copy-done.1
  (13 shorter events, 0.1 us)
Async XLA Ops:
  6.5 12.2 %copy-start = (bf16[16,128,512]{2,1,0:T(8,128)(2,1)S(1)}, bf16[16,128,512]{2,1,0:T(8,128)(2,1)}, u32[]{:S(2)}) copy-start(bf16[16,128,512]{2,1,0:T(8,128)(2,1)} %param.7) | copy-start | bytes 6291460
  8.0 15.6 %all-to-all-start = ((s32[8,128,2]{1,2,0:T(2,128)}), s32[8,128,2]{1,2,0:T(2,128)S(1)}, u32[]{:S(2)}, u32[]{:S(2)}) async-start(s32[8,128,2]{1,2,0:T(2,128)} %broadcast_in_dim.17), calls=%async_computation | async-start | bytes 16384 | tf_op jit(solution)/shard_map/all_to_all | solution.py:13
  15.9 112.8 %all-gather.2.cloned.1.call-start = ((), (), s32[]{:S(2)}) async-start(), calls=%async_computation.4 | async-start | bytes 15597568 | tf_op jit(solution)/shard_map/all_gather | solution.py:84
  49.5 246.4 %reduce-scatter.2.cloned.1.call-start = ((), (), s32[]{:S(2)}) async-start(), calls=%async_computation.5 | async-start | bytes 15597568 | tf_op jit(solution)/shard_map/reduce_scatter | solution.py:93
  205.8 99.3 %copy-start.2 = (f32[128]{0:T(128)S(1)}, f32[128]{0:T(128)}, u32[]{:S(2)}) copy-start(f32[128]{0:T(128)} %param.11) | copy-start | bytes 1540
  205.8 116.7 %copy-start.1 = (bf16[16,128,512]{2,1,0:T(8,128)(2,1)S(1)}, bf16[16,128,512]{2,1,0:T(8,128)(2,1)}, u32[]{:S(2)}) copy-start(bf16[16,128,512]{2,1,0:T(8,128)(2,1)} %param.7) | copy-start | bytes 6291460
  298.3 20.3 %all-to-all-start.2 = ((bf16[8,1,14,4096]{3,2,1,0:T(8,128)(2,1)}), bf16[8,1,14,4096]{3,2,1,0:T(8,128)(2,1)S(1)}, u32[]{:S(2)}, u32[]{:S(2)}) async-start(bf16[8,1,14,4096]{3,2,1,0:T(8,128)(2,1)} %bitcast.90), calls=%async_computation.3 | async-start | bytes 2097152 | tf_op jit(solution)/shard_map/all_to_all | solution.py:100
Sparse Core Ops, SparseCore 0:
  49.6 78.9 all-gather.1
  205.9 89.9 reduce-scatter.1
where the time goes:
time: 330 us; the launch traced here: 329 us
  waiting for transfers between devices  187 us (57%)
  local copies, waits for them, and re-layouts  45.2 us (14%)
  matrix products  44.8 us (14%)
  blocking collectives  18 us (5%)
  starting transfers between devices  14.9 us (5%)
  between operations  13.6 us (4%)
  other arithmetic  6.23 us (2%)
    reduce_scatter x1, waiting for transfers between devices, local(): lax.psum_scatter(partial_value.reshape(dev_rows * lax.axis_size('fsdp'),...  90.1 us
    all_gather x1, waiting for transfers between devices, local(): lax.all_gather(arrived[None], 'fsdp', axis=0, tiled=True)  78.9 us
    convert_element_type x2, local copies, waits for them, and re-layouts, local(): partial_value.reshape(dev_rows * lax.axis_size('fsdp'), model_width)  35.5 us
    dot_general x1, matrix products, local(): jnp.einsum('fbech,ehd->fbecd', hidden, down_weight, preferred_element_typ...  20.9 us
    dot_general x1, matrix products, local(): jnp.einsum('fbecd,ehd->fbech', lax.all_gather(arrived[None], 'fsdp', axis...  20.7 us
    all_to_all x1, blocking collectives, local(): lax.all_to_all(outgoing, 'expert', split_axis=1, concat_axis=4, tiled=True)  18 us
    all_to_all x1, waiting for transfers between devices, local(): lax.all_to_all(expert_out, 'expert', split_axis=0, concat_axis=1, tiled=T...  13.4 us
    all_to_all x1, starting transfers between devices, sent_to_all(): lax.all_to_all(jnp.broadcast_to(value[None], (length, *value.shape)), axi...  7.89 us
  transfers between devices with their start and end apart: 4, of which 4 were waited for; matrix products, arithmetic and copies ran while one was open for 1% of the time, Pallas kernels for 0%

commit v1 on v0

--- a/solution.py
+++ b/solution.py
@@ -1,11 +1,15 @@
 import jax
 import jax.numpy as jnp
 from jax import lax
+from jax.experimental import pallas as pl
+from jax.experimental.pallas import tpu as pltpu
 from jax.sharding import PartitionSpec as P
 
 EXPERTS = 8
 TOP = 2
 CAP = 14
+
+PARTS = (("A", 32), ("B", 32), ("A", 32), ("B", 16))
 
 
 def sent_to_all(value, axis):
@@ -56,6 +60,343 @@
     first_hit = (targets[:row_count, None] == slot_ids).astype(jnp.float32)
     second_hit = (targets[row_count:, None] == slot_ids).astype(jnp.float32)
     return first_hit * weight_first + second_hit * weight_second
+
+
+def layer_kernel(x_ref, gate_ref, down_ref, out_ref, gate_all, down_all, hid, *rest):
+    count = len(PARTS)
+    rows, partial, land = rest[:count], rest[count : 2 * count], rest[2 * count : 3 * count]
+    ag_send, ag_recv, rs_send, rs_recv, w_send, w_recv, w_local = rest[3 * count :]
+    width = x_ref.shape[1]
+    half = width // 2
+    own_hidden = gate_ref.shape[0]
+    hidden = 2 * own_hidden
+    starts = [sum(r for _, r in PARTS[:p]) for p in range(count)]
+
+    me = lax.axis_index("fsdp")
+    core = me % 2
+    y = (me // 2) % 4
+    x = me // 8
+    xn = (1 - x) * 8 + y * 2 + core
+    yp = x * 8 + ((y + 1) % 4) * 2 + core
+    ym = x * 8 + ((y + 3) % 4) * 2 + core
+    cn = x * 8 + y * 2 + 1 - core
+
+    barrier = pltpu.get_barrier_semaphore()
+    for dev in (xn, yp, ym, cn):
+        pl.semaphore_signal(
+            barrier, inc=1, device_id={"fsdp": dev}, device_id_type=pl.DeviceIdType.MESH
+        )
+    pl.semaphore_wait(barrier, 4)
+
+    def remote(src, dst, send_sem, recv_sem, dev):
+        return pltpu.make_async_remote_copy(
+            src_ref=src,
+            dst_ref=dst,
+            send_sem=send_sem,
+            recv_sem=recv_sem,
+            device_id={"fsdp": dev},
+            device_id_type=pl.DeviceIdType.MESH,
+        )
+
+    weights = []
+    for k, (src, dst) in enumerate(((gate_ref, gate_all), (down_ref, down_all))):
+        local = pltpu.make_async_copy(src, dst.at[pl.ds(0, own_hidden)], w_local.at[k])
+        other = remote(
+            src, dst.at[pl.ds(own_hidden, own_hidden)], w_send.at[k], w_recv.at[k], cn
+        )
+        weights.append((local, other))
+
+    LEFT, RIGHT, FULL = pl.ds(0, half), pl.ds(half, half), pl.ds(0, width)
+
+    gathers, reduces = [], []
+    for p, (kind, size) in enumerate(PARTS):
+        own = x_ref.at[pl.ds(starts[p], size)]
+        names = {}
+
+        def view(ref, index, cols, size=size):
+            return ref.at[pl.ds(index * size, size), cols]
+
+        def gather(name, src, index, cols, dev, p=p, names=names, view=view):
+            n = len(names)
+            source = own if src is None else view(rows[p], src, cols)
+            names[name] = remote(
+                source, view(rows[p], index, cols), ag_send.at[p * 9 + n], ag_recv.at[p * 9 + n], dev
+            )
+
+        gather("p0", None, 3, FULL, yp)
+        gather("m0", None, 1, FULL, ym)
+        gather("x0", None, 4, FULL, xn)
+        gather("ph0", 3, 2, LEFT, yp)
+        gather("mh0", 1, 2, RIGHT, ym)
+        if kind == "A":
+            gather("p1", 4, 7, FULL, yp)
+            gather("m1", 4, 5, FULL, ym)
+            gather("ph1", 7, 6, LEFT, yp)
+            gather("mh1", 5, 6, RIGHT, ym)
+        else:
+            gather("x3", 3, 7, FULL, xn)
+            gather("x1", 1, 5, FULL, xn)
+            gather("x2", 2, 6, FULL, xn)
+        gathers.append(names)
+
+        sums = {}
+
+        def reduce(name, src, index, cols, dev, p=p, sums=sums, view=view):
+            n = len(sums)
+            sums[name] = remote(
+                view(partial[p], src, cols),
+                view(land[p], index, cols),
+                rs_send.at[p * 9 + n],
+                rs_recv.at[p * 9 + n],
+                dev,
+            )
+
+        if kind == "A":
+            for rx in (0, 1):
+                reduce(f"hp{rx}", rx * 4 + 2, rx, LEFT, yp)
+                reduce(f"hm{rx}", rx * 4 + 2, rx, RIGHT, ym)
+                reduce(f"fp{rx}", rx * 4 + 1, 2 + 2 * rx, FULL, yp)
+                reduce(f"fm{rx}", rx * 4 + 3, 3 + 2 * rx, FULL, ym)
+            reduce("x", 4, 6, FULL, xn)
+        else:
+            for ry in range(4):
+                reduce(f"x{ry}", 4 + ry, ry, FULL, xn)
+            reduce("hp", 2, 4, LEFT, yp)
+            reduce("hm", 2, 4, RIGHT, ym)
+            reduce("fp", 1, 5, FULL, yp)
+            reduce("fm", 3, 6, FULL, ym)
+        reduces.append(sums)
+
+    def ag(p, stage):
+        kind = PARTS[p][0]
+        m = gathers[p]
+
+        def begin(*keys):
+            for key in keys:
+                m[key].start()
+
+        def got(*keys):
+            for key in keys:
+                m[key].wait_recv()
+
+        if stage == 0:
+            begin("p0", "m0", "x0")
+            size = PARTS[p][1]
+            rows[p][pl.ds(0, size), :] = x_ref[pl.ds(starts[p], size), :]
+        elif kind == "A":
+            if stage == 1:
+                got("p0")
+                begin("ph0")
+                got("m0")
+                begin("mh0")
+                got("x0")
+                begin("p1", "m1")
+            elif stage == 2:
+                got("p1")
+                begin("ph1")
+                got("m1")
+                begin("mh1")
+            else:
+                got("ph0", "mh0", "ph1", "mh1")
+        else:
+            if stage == 1:
+                got("p0")
+                begin("ph0", "x3")
+                got("m0")
+                begin("mh0", "x1")
+            elif stage == 2:
+                got("ph0", "mh0")
+                begin("x2")
+            else:
+                got("x0", "x3", "x1", "x2")
+
+    CHUNK = 512
+
+    def add(p, index, terms, into=None):
+        size = PARTS[p][1]
+        spans = {}
+        for at, cols in terms:
+            for c in range(0, width, half):
+                if cols is FULL or (cols is LEFT) == (c == 0):
+                    spans.setdefault(c, []).append(at)
+        for c, ats in spans.items():
+
+            def body(i, carry, c=c, ats=ats):
+                cols = pl.ds(pl.multiple_of(c + i * CHUNK, CHUNK), CHUNK)
+                total = partial[p][pl.ds(index * size, size), cols].astype(jnp.float32)
+                for at in ats:
+                    total = total + land[p][pl.ds(at * size, size), cols].astype(jnp.float32)
+                total = total.astype(jnp.bfloat16)
+                if into is None:
+                    partial[p][pl.ds(index * size, size), cols] = total
+                else:
+                    into[pl.ds(starts[p], size), cols] = total
+                return carry
+
+            lax.fori_loop(0, half // CHUNK, body, 0)
+
+    def rs(p, stage):
+        kind = PARTS[p][0]
+        m = reduces[p]
+
+        def begin(*keys):
+            for key in keys:
+                m[key].start()
+
+        def got(*keys):
+            for key in keys:
+                m[key].wait_recv()
+
+        if kind == "A":
+            if stage == 0:
+                begin("hp0", "hm0", "hp1", "hm1")
+            elif stage == 1:
+                for rx in (1, 0):
+                    got(f"hp{rx}")
+                    add(p, rx * 4 + 1, [(rx, LEFT)])
+                    begin(f"fp{rx}")
+                    got(f"hm{rx}")
+                    add(p, rx * 4 + 3, [(rx, RIGHT)])
+                    begin(f"fm{rx}")
+            elif stage == 2:
+                got("fp1", "fm1")
+                add(p, 4, [(4, FULL), (5, FULL)])
+                begin("x")
+            else:
+                got("fp0", "fm0", "x")
+                add(p, 0, [(2, FULL), (3, FULL), (6, FULL)], out_ref)
+        else:
+            if stage == 0:
+                begin("x2", "x1", "x3", "x0")
+            elif stage == 1:
+                got("x2")
+                add(p, 2, [(2, FULL)])
+                begin("hp", "hm")
+            elif stage == 2:
+                got("x1", "hp")
+                add(p, 1, [(1, FULL), (4, LEFT)])
+                begin("fp")
+                got("x3", "hm")
+                add(p, 3, [(3, FULL), (4, RIGHT)])
+                begin("fm")
+            else:
+                got("x0", "fp", "fm")
+                add(p, 0, [(0, FULL), (5, FULL), (6, FULL)], out_ref)
+
+    TILE = 256
+
+    def compute(p, gate_hooks=(), down_hooks=(), before_down=None):
+        size = 8 * PARTS[p][1]
+
+        def gate_body(i, carry):
+            span = pl.ds(pl.multiple_of(i * TILE, TILE), TILE)
+            act = lax.dot_general(
+                rows[p][...],
+                gate_all[span, :],
+                (((1,), (1,)), ((), ())),
+                preferred_element_type=jnp.float32,
+            )
+            hid[pl.ds(0, size), span] = (act / (1.0 + jnp.exp(-act))).astype(jnp.bfloat16)
+            for at, hook in gate_hooks:
+                pl.when(i == at)(hook)
+            return carry
+
+        lax.fori_loop(0, hidden // TILE, gate_body, 0)
+        if before_down is not None:
+            before_down()
+
+        def down_body(i, carry):
+            span = pl.ds(pl.multiple_of(i * TILE, TILE), TILE)
+            value = jnp.dot(
+                hid[pl.ds(0, size), :], down_all[:, span], preferred_element_type=jnp.float32
+            )
+            partial[p][:, span] = value.astype(jnp.bfloat16)
+            for at, hook in down_hooks:
+                pl.when(i == at)(hook)
+            return carry
+
+        lax.fori_loop(0, width // TILE, down_body, 0)
+
+    def step(fn, *args):
+        return lambda: fn(*args)
+
+    ag(0, 0)
+    for local, other in weights:
+        other.start()
+        local.start()
+    ag(1, 0)
+    ag(0, 1)
+    ag(2, 0)
+    ag(1, 1)
+    ag(0, 2)
+    ag(3, 0)
+    ag(2, 1)
+    ag(1, 2)
+    ag(0, 3)
+
+    def weights_here(k):
+        weights[k][0].wait()
+        weights[k][1].wait_recv()
+
+    weights_here(0)
+    compute(
+        0,
+        [(1, step(ag, 3, 1)), (4, step(ag, 2, 2))],
+        [(1, step(ag, 3, 2))],
+        lambda: weights_here(1),
+    )
+    rs(0, 0)
+    ag(1, 3)
+    compute(1, [(1, step(rs, 0, 1)), (5, step(rs, 0, 2))], [(10, step(rs, 0, 3))])
+    rs(1, 0)
+    ag(2, 3)
+    compute(2, [(2, step(rs, 1, 1))], [(0, step(rs, 1, 2)), (12, step(rs, 1, 3))])
+    rs(2, 0)
+    ag(3, 3)
+    compute(3, [(3, step(rs, 2, 1))], [(6, step(rs, 2, 2))])
+    rs(3, 0)
+    rs(2, 3)
+    rs(3, 1)
+    rs(3, 2)
+    rs(3, 3)
+    for _, other in weights:
+        other.wait_send()
+    for names in (*gathers, *reduces):
+        for copy in names.values():
+            copy.wait_send()
+
+
+def run_layer(x, gate, down):
+    total, width = x.shape
+    hidden = 2 * gate.shape[0]
+    most = max(r for _, r in PARTS)
+    count = len(PARTS)
+    bf16 = jnp.bfloat16
+    scratch = [
+        pltpu.VMEM((hidden, width), bf16),
+        pltpu.VMEM((hidden, width), bf16),
+        pltpu.VMEM((8 * most, hidden), bf16),
+    ]
+    scratch += [pltpu.VMEM((8 * r, width), bf16) for _, r in PARTS]
+    scratch += [pltpu.VMEM((8 * r, width), bf16) for _, r in PARTS]
+    scratch += [pltpu.VMEM((7 * r, width), bf16) for _, r in PARTS]
+    scratch += [pltpu.SemaphoreType.DMA((9 * count,)) for _ in range(4)]
+    scratch += [pltpu.SemaphoreType.DMA((2,)) for _ in range(3)]
+    return pl.pallas_call(
+        layer_kernel,
+        out_shape=jax.ShapeDtypeStruct((total, width), bf16),
+        in_specs=[
+            pl.BlockSpec(memory_space=pltpu.VMEM),
+            pl.BlockSpec(memory_space=pl.ANY),
+            pl.BlockSpec(memory_space=pl.ANY),
+        ],
+        out_specs=pl.BlockSpec(memory_space=pltpu.VMEM),
+        scratch_shapes=scratch,
+        compiler_params=pltpu.CompilerParams(
+            collective_id=0, has_side_effects=True, vmem_limit_bytes=67043328
+        ),
+        name="layer",
+    )(x, gate, down)
 
 
 def local(pool, picks, lengths, routes, route_gap, gate_weight, down_weight):
@@ -77,25 +418,9 @@
     ).astype(jnp.bfloat16)
     outgoing = outgoing.reshape(expert_count, expert_count, expert_local, CAP, selected.shape[2])
     arrived = lax.all_to_all(outgoing, "expert", split_axis=1, concat_axis=4, tiled=True)
-    arrived = arrived.reshape(expert_count, expert_local, CAP, model_width)
     my_targets = lax.dynamic_index_in_dim(all_targets, my_column, 0, keepdims=False)
-    gate_act = jnp.einsum(
-        "fbecd,ehd->fbech",
-        lax.all_gather(arrived[None], "fsdp", axis=0, tiled=True),
-        gate_weight,
-        preferred_element_type=jnp.float32,
-    )
-    hidden = jax.nn.silu(gate_act).astype(jnp.bfloat16)
     dev_rows = expert_count * expert_local * CAP
-    partial_value = jnp.einsum(
-        "fbech,ehd->fbecd", hidden, down_weight, preferred_element_type=jnp.float32
-    )
-    summed = lax.psum_scatter(
-        partial_value.reshape(dev_rows * lax.axis_size("fsdp"), model_width).astype(jnp.bfloat16),
-        "fsdp",
-        scatter_dimension=0,
-        tiled=True,
-    )
+    summed = run_layer(arrived.reshape(dev_rows, model_width), gate_weight[0], down_weight[0])
     expert_out = summed.reshape(expert_count, expert_local, CAP, model_width)
     returned = lax.all_to_all(expert_out, "expert", split_axis=0, concat_axis=1, tiled=True)
     flat_out = returned.reshape(EXPERTS * CAP, model_width).astype(jnp.float32)

time: 330 us -> 202 us (0.61)
  waiting for transfers between devices: 187 us -> 13.7 us
  Pallas kernels: 0 us -> 137 us
  matrix products: 44.8 us -> 1.95 us
  local copies, waits for them, and re-layouts: 45.2 us -> 10.8 us
  between operations: 13.6 us -> 0.18 us
  starting transfers between devices: 14.9 us -> 11.4 us
    pallas_call x0 -> x1, Pallas kernels: none -> 137 us  [run_layer(): pl.pallas_call(layer_kernel, out_shape=jax.ShapeDtypeStruct((total, width...]
    reduce_scatter x1 -> x0, waiting for transfers between devices: 90.1 us -> none  [local(): lax.psum_scatter(partial_value.reshape(dev_rows * lax.axis_size('fsdp'),...]
    all_gather x1 -> x0, waiting for transfers between devices: 78.9 us -> none  [local(): lax.all_gather(arrived[None], 'fsdp', axis=0, tiled=True)]
    dot_general x2 -> x0, matrix products: 41.6 us -> none  [the longest x1 20.9 us: local(): jnp.einsum('fbech,ehd->fbecd', hidden, down_weight, preferred_element_typ...]
    convert_element_type x2 -> x0, local copies, waits for them, and re-layouts: 35.5 us -> none  [local(): partial_value.reshape(dev_rows * lax.axis_size('fsdp'), model_width)]
  transfers between devices with their start and end apart: 4 -> 2, of which waited for: 4 -> 2; matrix products, arithmetic and copies ran while one was open for 1% -> 3% of each run, Pallas kernels for 0% -> 0%
where the time goes in v1:
time: 202 us; the launch traced here: 201 us
  Pallas kernels  137 us (68%)
  blocking collectives  19.6 us (10%)
  waiting for transfers between devices  13.7 us (7%)
  starting transfers between devices  11.4 us (6%)
  local copies, waits for them, and re-layouts  10.8 us (5%)
  other arithmetic  6.22 us (3%)
    pallas_call x1, Pallas kernels, run_layer(): pl.pallas_call(layer_kernel, out_shape=jax.ShapeDtypeStruct((total, width...  137 us
    all_to_all x1, blocking collectives, local(): lax.all_to_all(outgoing, 'expert', split_axis=1, concat_axis=4, tiled=True)  19.6 us
    all_to_all x1, waiting for transfers between devices, local(): lax.all_to_all(expert_out, 'expert', split_axis=0, concat_axis=1, tiled=T...  11 us
    all_to_all x1, starting transfers between devices, sent_to_all(): lax.all_to_all(jnp.broadcast_to(value[None], (length, *value.shape)), axi...  7.89 us
    another operation x2, other arithmetic  4.58 us
  transfers between devices with their start and end apart: 2, of which 2 were waited for; matrix products, arithmetic and copies ran while one was open for 3% of the time, Pallas kernels for 0%

profile of v1, /device:TPU:0, one launch (start us, length us, event | category | flops | bytes accessed | tf_op | source)
XLA Modules:
  0.0 201.4 jit_solution(5625848145615833604)
XLA Ops:
  0.0 1.3 broadcast_in_dim.17
  1.3 7.9 %all-to-all-start = ((s32[8,128,2]{1,2,0:T(2,128)}), s32[8,128,2]{1,2,0:T(2,128)S(1)}, u32[]{:S(2)}, u32[]{:S(2)}) async-start(s32[8,128,2]{1,2,0:T(2,128)} %broadcast_in_dim.17), calls=%async_computation | async-start | bytes 16384 | tf_op jit(solution)/shard_map/all_to_all | solution.py:17
  9.2 0.7 fusion.22
  9.8 1.3 gather_fusion
  11.1 0.7 broadcast_select_fusion
  11.8 0.1 iota_compare_fusion.10
  11.9 0.1 iota_compare_fusion.9
  12.0 2.2 %gather_fusion.1 = bf16[8,128,512]{2,1,0:T(8,128)(2,1)S(1)} fusion(bf16[16,128,512]{2,1,0:T(8,128)(2,1)} %param.7, s32[1024]{0:T(1024)S(1)} %pad_clamp_fusion), kind=kCustom, calls=%fused_computation.1 | custom fusion | bytes 2097184 | tf_op jit(solution)/shard_map/jit(_take)/gather | solution.py:409
  14.2 2.7 %all-to-all-done = s32[8,128,2]{1,2,0:T(2,128)S(1)} async-done(((s32[8,128,2]{1,2,0:T(2,128)}), s32[8,128,2]{1,2,0:T(2,128)S(1)}, u32[]{:S(2)}, u32[]{:S(2)}) %all-to-all-start) | async-done | bytes 8224 | tf_op jit(solution)/shard_map/all_to_all | solution.py:17
  16.9 4.5 %reduce-window.6 = s32[8,8,2,128]{3,1,2,0:T(8,128)S(1)} reduce-window(s32[8,8,2,128]{3,1,2,0:T(8,128)S(1)} %fusion.14, s32[]{:T(128)} %constant.33.clone.1), window={size=1x1x1x128 pad=0_0x0_0x0_0x127_0}, to_apply=%region_0.1 | reduce-window | flops 2080768 | bytes 131076 | tf_op jit(solution)/shard_map/reduce-window
  21.4 0.1 slice.40
  21.5 0.2 copy.19
  21.7 0.1 fusion.20
  21.8 0.1 fusion.8
  21.9 0.0 copy-start
  21.9 0.5 convolution_convert_fusion.1
  22.4 0.5 copy.21
  22.9 19.6 %all_to_all.29 = bf16[8,8,1,14,512]{4,0,3,2,1:T(8,128)(2,1)S(1)} all-to-all(bf16[8,8,1,14,512]{4,0,3,2,1:T(8,128)(2,1)S(1)} %bitcast.45), channel_id=1, replica_groups=mesh['fsdp'=16,'expert'=8] {'expert'}, dimensions={1} | all-to-all | bytes 1835008 | tf_op jit(solution)/shard_map/all_to_all | solution.py:420
  42.5 0.0 copy-done
  42.5 0.5 copy.23
  43.0 1.2 copy.26
  44.3 137.5 %layer.1 = bf16[112,4096]{1,0:T(8,128)(2,1)} custom-call(bf16[112,4096]{1,0:T(8,128)(2,1)} %bitcast.48, bf16[896,4096]{1,0:T(8,128)(2,1)} %bitcast.43, bf16[896,4096]{1,0:T(8,128)(2,1)} %bitcast.44), custom_call_target="tpu_custom_call" | custom-call | tf_op jit(solution)/shard_map/layer/pallas_call | solution.py:385
  181.8 0.0 copy-start.1
  181.8 2.4 %reshape.135 = bf16[8,1,14,4096]{3,2,0,1:T(8,128)(2,1)} reshape(bf16[112,4096]{1,0:T(8,128)(2,1)} %layer.1) | data formatting | bytes 1835008 | tf_op jit(solution)/shard_map/reshape | solution.py:424
  184.2 3.6 %all-to-all-start.2 = ((bf16[8,1,14,4096]{3,2,1,0:T(8,128)(2,1)}), bf16[8,1,14,4096]{3,2,1,0:T(8,128)(2,1)S(1)}, u32[]{:S(2)}, u32[]{:S(2)}) async-start(bf16[8,1,14,4096]{3,2,1,0:T(8,128)(2,1)} %bitcast.18), calls=%async_computation.2 | async-start | bytes 2097152 | tf_op jit(solution)/shard_map/all_to_all | solution.py:425
  187.8 0.0 copy-done.1
  187.8 0.8 dynamic-slice_bitcast_fusion.1
  188.6 11.0 %all-to-all-done.2 = bf16[8,1,14,4096]{3,2,1,0:T(8,128)(2,1)S(1)} async-done(((bf16[8,1,14,4096]{3,2,1,0:T(8,128)(2,1)}), bf16[8,1,14,4096]{3,2,1,0:T(8,128)(2,1)S(1)}, u32[]{:S(2)}, u32[]{:S(2)}) %all-to-all-start.2) | async-done | bytes 917536 | tf_op jit(solution)/shard_map/all_to_all | solution.py:425
  199.6 0.3 reshape.136
  199.9 1.5 convolution_convert_fusion
  (13 shorter events, 0.1 us)
Async XLA Ops:
  1.3 15.6 %all-to-all-start = ((s32[8,128,2]{1,2,0:T(2,128)}), s32[8,128,2]{1,2,0:T(2,128)S(1)}, u32[]{:S(2)}, u32[]{:S(2)}) async-start(s32[8,128,2]{1,2,0:T(2,128)} %broadcast_in_dim.17), calls=%async_computation | async-start | bytes 16384 | tf_op jit(solution)/shard_map/all_to_all | solution.py:17
  21.9 20.6 %copy-start = (s32[8,256]{1,0:T(8,128)}, s32[8,256]{1,0:T(8,128)S(1)}, u32[]{:S(2)}) copy-start(s32[8,256]{1,0:T(8,128)S(1)} %add_select_fusion) | copy-start | bytes 24580
  181.8 6.0 %copy-start.1 = (f32[128]{0:T(128)S(1)}, f32[128]{0:T(128)}, u32[]{:S(2)}) copy-start(f32[128]{0:T(128)} %param.11) | copy-start | bytes 1540
  184.2 15.4 %all-to-all-start.2 = ((bf16[8,1,14,4096]{3,2,1,0:T(8,128)(2,1)}), bf16[8,1,14,4096]{3,2,1,0:T(8,128)(2,1)S(1)}, u32[]{:S(2)}, u32[]{:S(2)}) async-start(bf16[8,1,14,4096]{3,2,1,0:T(8,128)(2,1)} %bitcast.18), calls=%async_computation.2 | async-start | bytes 2097152 | tf_op jit(solution)/shard_map/all_to_all | solution.py:425

commit v2 on v1

v2 whole, which is shorter than its diff:
```python
import jax
import jax.numpy as jnp
from jax import lax
from jax.experimental import pallas as pl
from jax.experimental.pallas import tpu as pltpu
from jax.sharding import PartitionSpec as P

EXPERTS = 8
CAP = 14
WIN = 128

PARTS = (("A", 32), ("B", 32), ("A", 32), ("B", 16))
COUNT = len(PARTS)
STARTS = tuple(sum(r for _, r in PARTS[:p]) for p in range(COUNT))
TILE = 256
CHUNK = 512
NOWHERE = -4096


def layer_kernel(
    picks_ref, lengths_ref, routes_ref, gap_ref, pool_ref, gate_ref, down_ref, out_ref, *rest
):
    gate_all, down_all, hid, keys, tokens, back_a, back_b = rest[:7]
    rest = rest[7:]
    rows, partial, land, ready, summed, packed = (
        rest[k * COUNT : (k + 1) * COUNT] for k in range(6)
    )
    (
        ag_send, ag_recv, rs_send, rs_recv, w_send, w_recv, w_local,
        key_send, key_recv, go_send, go_recv, ret_send, ret_recv,
    ) = rest[6 * COUNT :]
    f32, bf16, i32 = jnp.float32, jnp.bfloat16, jnp.int32
    width = out_ref.shape[1]
    half = width // 2
    feats = pool_ref.shape[2]
    own_hidden = gate_ref.shape[0]
    hidden = 2 * own_hidden

    me = lax.axis_index("fsdp")
    col = lax.axis_index("expert")
    core = me % 2
    y = (me // 2) % 4
    x = me // 8
    z = col % 4
    xh = col // 4
    xn = (1 - x) * 8 + y * 2 + core
    yp = x * 8 + ((y + 1) % 4) * 2 + core
    ym = x * 8 + ((y + 3) % 4) * 2 + core
    cn = x * 8 + y * 2 + 1 - core

    def column(dx, dz):
        return (xh if dx == 0 else 1 - xh) * 4 + (z + dz) % 4

    others = [(dx, dz) for dz in (2, 1, 3, 0) for dx in (1, 0) if dx or dz]

    def plane(dev):
        return {"fsdp": dev, "expert": col}

    def same(dx, dz):
        return {"fsdp": me, "expert": column(dx, dz)}

    def crossed(dx, dz):
        return {"fsdp": xn if dx else me, "expert": column(dx, dz)}

    barrier = pltpu.get_barrier_semaphore()
    greeted = [plane(dev) for dev in (xn, yp, ym, cn)]
    greeted += [same(dx, dz) for dx, dz in others]
    greeted += [crossed(dx, dz) for dx, dz in others if dx]
    for dev in greeted:
        pl.semaphore_signal(barrier, inc=1, device_id=dev, device_id_type=pl.DeviceIdType.MESH)

    length = lengths_ref[picks_ref[0, col]]
    lane = lax.broadcasted_iota(i32, (EXPERTS, WIN), 1)
    expert_of = lax.broadcasted_iota(i32, (EXPERTS, WIN), 0)
    live = lane < length
    before = (
        lax.broadcasted_iota(i32, (WIN, WIN), 0) < lax.broadcasted_iota(i32, (WIN, WIN), 1)
    ).astype(bf16)
    ids = [routes_ref[k : k + 1, :] for k in (0, 1)]
    hits = [jnp.where((expert_of == ids[k]) & live, 1.0, 0.0) for k in (0, 1)]
    earlier = [jnp.dot(hit.astype(bf16), before, preferred_element_type=f32) for hit in hits]
    earlier[1] = earlier[1] + jnp.sum(hits[0], axis=1, keepdims=True)
    key_rows, code_rows = [], []
    for k in (0, 1):
        rank = jnp.sum(hits[k] * earlier[k], axis=0, keepdims=True).astype(i32)
        kept = (lane[:1] < length) & (rank < CAP)
        low = rank < 12
        split = jnp.where(xh == ids[k] // 4, 0, 1)
        key = jnp.where(
            low,
            (rank // 4) * 256 + ids[k] * 32 + split * 16 + z * 4 + rank % 4,
            768 + ids[k] * 16 + split * 8 + z * 2 + rank - 12,
        )
        key_rows.append(jnp.where(kept, key, NOWHERE))
        code_rows.append(
            jnp.where(kept & low, (rank // 4) * 128 + ids[k] * 16 + (rank % 4) * 4, NOWHERE)
        )
        code_rows.append(jnp.where(kept & (rank >= 12), ids[k] * 16 + (rank - 12) * 8, NOWHERE))
    key_block = jnp.concatenate(
        [key_rows[0], key_rows[1], jnp.full((6, WIN), NOWHERE, i32)], axis=0
    )
    keys[col] = key_block

    pl.semaphore_wait(barrier, len(greeted))

    sent = []

    def remote(src, dst, send_sem, recv_sem, dev):
        copy = pltpu.make_async_remote_copy(
            src_ref=src,
            dst_ref=dst,
            send_sem=send_sem,
            recv_sem=recv_sem,
            device_id=dev,
            device_id_type=pl.DeviceIdType.MESH,
        )
        sent.append(copy)
        return copy

    key_copies = [
        remote(keys.at[col], keys.at[col], key_send.at[n], key_recv.at[n], same(dx, dz))
        for n, (dx, dz) in enumerate(others)
    ]
    for copy in key_copies:
        copy.start()

    weights = []
    for k, (src, dst) in enumerate(((gate_ref, gate_all), (down_ref, down_all))):
        kept_half = pltpu.make_async_copy(src, dst.at[pl.ds(0, own_hidden)], w_local.at[k])
        other = remote(
            src, dst.at[pl.ds(own_hidden, own_hidden)], w_send.at[k], w_recv.at[k], plane(cn)
        )
        weights.append((kept_half, other))
        other.start()
        kept_half.start()

    LEFT, RIGHT, FULL = pl.ds(0, half), pl.ds(half, half), pl.ds(0, width)

    gathers, reduces, goes, returns = [], [], [], []
    for p, (kind, size) in enumerate(PARTS):
        names = {}

        def view(ref, index, cols, size=size):
            return ref.at[pl.ds(index * size, size), cols]

        def gather(name, src, index, cols, dev, p=p, names=names, view=view):
            n = p * 9 + len(names)
            names[name] = remote(
                view(rows[p], src, cols), view(rows[p], index, cols),
                ag_send.at[n], ag_recv.at[n], plane(dev),
            )

        gather("p0", 0, 3, FULL, yp)
        gather("m0", 0, 1, FULL, ym)
        gather("x0", 0, 4, FULL, xn)
        gather("ph0", 3, 2, LEFT, yp)
        gather("mh0", 1, 2, RIGHT, ym)
        if kind == "A":
            gather("p1", 4, 7, FULL, yp)
            gather("m1", 4, 5, FULL, ym)
            gather("ph1", 7, 6, LEFT, yp)
            gather("mh1", 5, 6, RIGHT, ym)
        else:
            gather("x3", 3, 7, FULL, xn)
            gather("x1", 1, 5, FULL, xn)
            gather("x2", 2, 6, FULL, xn)
        gathers.append(names)

        sums = {}

        def reduce(name, src, index, cols, dev, p=p, sums=sums, view=view):
            n = p * 9 + len(sums)
            sums[name] = remote(
                view(partial[p], src, cols), view(land[p], index, cols),
                rs_send.at[n], rs_recv.at[n], plane(dev),
            )

        if kind == "A":
            for rx in (0, 1):
                reduce(f"hp{rx}", rx * 4 + 2, rx, LEFT, yp)
                reduce(f"hm{rx}", rx * 4 + 2, rx, RIGHT, ym)
                reduce(f"fp{rx}", rx * 4 + 1, 2 + 2 * rx, FULL, yp)
                reduce(f"fm{rx}", rx * 4 + 3, 3 + 2 * rx, FULL, ym)
            reduce("x", 4, 6, FULL, xn)
        else:
            for ry in range(4):
                reduce(f"x{ry}", 4 + ry, ry, FULL, xn)
            reduce("hp", 2, 4, LEFT, yp)
            reduce("hm", 2, 4, RIGHT, ym)
            reduce("fp", 1, 5, FULL, yp)
            reduce("fm", 3, 6, FULL, ym)
        reduces.append(sums)

        goes.append(
            [
                remote(
                    ready[p].at[pl.ds(pl.multiple_of(column(dx, dz) * size, size), size)],
                    rows[p].at[
                        pl.ds(0, size), pl.ds(pl.multiple_of(dx * half + z * feats, feats), feats)
                    ],
                    go_send.at[p * 7 + n], go_recv.at[p * 7 + n], crossed(dx, dz),
                )
                for n, (dx, dz) in enumerate(others)
            ]
        )
        back = back_a.at[pl.ds(p * 128, 128)] if size == 32 else back_b
        returns.append(
            [
                remote(
                    packed[p].at[pl.ds(pl.multiple_of((dx * 4 + (z + dz) % 4) * 16, 16), 16)],
                    back.at[pl.ds(pl.multiple_of(col * 16, 16), 16)],
                    ret_send.at[p * 7 + n], ret_recv.at[p * 7 + n], crossed(dx, dz),
                )
                for n, (dx, dz) in enumerate(others)
            ]
        )

    for b in range(EXPERTS):
        tokens[pl.ds(b * WIN, WIN), :] = pool_ref[picks_ref[0, b]]
    for copy in key_copies:
        copy.wait_recv()
    all_keys = [
        jnp.concatenate([keys[b, k : k + 1, :] for b in range(EXPERTS)], axis=1) for k in (0, 1)
    ]

    def dispatch(p):
        size = PARTS[p][1]
        slot = lax.broadcasted_iota(i32, (8 * size, EXPERTS * WIN), 0) + 8 * STARTS[p]
        table = jnp.where((slot == all_keys[0]) | (slot == all_keys[1]), 1.0, 0.0).astype(bf16)
        ready[p][...] = jnp.dot(table, tokens[...], preferred_element_type=f32).astype(bf16)
        for copy in goes[p]:
            copy.start()
        rows[p][pl.ds(0, size), pl.ds(pl.multiple_of(z * feats, feats), feats)] = ready[p][
            pl.ds(pl.multiple_of(col * size, size), size), :
        ]

    def steps(copies):
        def begin(*names):
            for name in names:
                copies[name].start()

        def got(*names):
            for name in names:
                copies[name].wait_recv()

        return begin, got

    def ag(p, stage):
        begin, got = steps(gathers[p])
        if stage == 0:
            for copy in goes[p]:
                copy.wait_recv()
            begin("p0", "m0", "x0")
        elif PARTS[p][0] == "A":
            if stage == 1:
                got("p0")
                begin("ph0")
                got("m0")
                begin("mh0")
                got("x0")
                begin("p1", "m1")
            elif stage == 2:
                got("p1")
                begin("ph1")
                got("m1")
                begin("mh1")
            else:
                got("ph0", "mh0", "ph1", "mh1")
        else:
            if stage == 1:
                got("p0")
                begin("ph0", "x3")
                got("m0")
                begin("mh0", "x1")
            elif stage == 2:
                got("ph0", "mh0")
                begin("x2")
            else:
                got("x0", "x3", "x1", "x2")

    def add(p, index, terms, last=False):
        size = PARTS[p][1]
        block = summed[p].shape[1]
        spans = {}
        for at, cols in terms:
            for c in range(0, width, half):
                if cols is FULL or (cols is LEFT) == (c == 0):
                    spans.setdefault(c, []).append(at)
        for c, ats in spans.items():

            def body(i, carry, c=c, ats=ats):
                cols = pl.ds(pl.multiple_of(c + i * CHUNK, CHUNK), CHUNK)
                total = partial[p][pl.ds(index * size, size), cols].astype(f32)
                for at in ats:
                    total = total + land[p][pl.ds(at * size, size), cols].astype(f32)
                total = total.astype(bf16)
                if last:
                    n = c // CHUNK + i
                    per = block // CHUNK
                    to = pl.ds(pl.multiple_of((n // per) * size, size), size)
                    summed[p][to, pl.ds(pl.multiple_of((n % per) * CHUNK, CHUNK), CHUNK)] = total
                else:
                    partial[p][pl.ds(index * size, size), cols] = total
                return carry

            lax.fori_loop(0, half // CHUNK, body, 0)

    def ret(p):
        size = PARTS[p][1]
        per = 128 // size
        j = lax.broadcasted_iota(i32, (128, 128), 0)
        i = lax.broadcasted_iota(i32, (128, 128), 1)
        order = jnp.where((j % per) * size + j // per == i, 1.0, 0.0).astype(bf16)
        packed[p][...] = jnp.dot(order, summed[p][...], preferred_element_type=f32).astype(bf16)
        for copy in returns[p]:
            copy.start()
        mine = packed[p][pl.ds(pl.multiple_of(z * 16, 16), 16), :]
        if size == 32:
            back_a[pl.ds(pl.multiple_of(p * 128 + col * 16, 16), 16), :] = mine
        else:
            back_b[pl.ds(pl.multiple_of(col * 16, 16), 16), :] = mine

    def rs(p, stage):
        begin, got = steps(reduces[p])
        if PARTS[p][0] == "A":
            if stage == 0:
                begin("hp0", "hm0", "hp1", "hm1")
            elif stage == 1:
                for rx in (1, 0):
                    got(f"hp{rx}")
                    add(p, rx * 4 + 1, [(rx, LEFT)])
                    begin(f"fp{rx}")
                    got(f"hm{rx}")
                    add(p, rx * 4 + 3, [(rx, RIGHT)])
                    begin(f"fm{rx}")
            elif stage == 2:
                got("fp1", "fm1")
                add(p, 4, [(4, FULL), (5, FULL)])
                begin("x")
            else:
                got("fp0", "fm0", "x")
                add(p, 0, [(2, FULL), (3, FULL), (6, FULL)], True)
                ret(p)
        else:
            if stage == 0:
                begin("x2", "x1", "x3", "x0")
            elif stage == 1:
                got("x2")
                add(p, 2, [(2, FULL)])
                begin("hp", "hm")
            elif stage == 2:
                got("x1", "hp")
                add(p, 1, [(1, FULL), (4, LEFT)])
                begin("fp")
                got("x3", "hm")
                add(p, 3, [(3, FULL), (4, RIGHT)])
                begin("fm")
            else:
                got("x0", "fp", "fm")
                add(p, 0, [(0, FULL), (5, FULL), (6, FULL)], True)
                ret(p)

    def compute(p, gate_hooks=(), down_hooks=(), before_down=None):
        size = PARTS[p][1]
        total = 8 * size
        near = pl.ds(pl.multiple_of(xh * half, half), half)
        far = pl.ds(pl.multiple_of((1 - xh) * half, half), half)
        contract = (((1,), (1,)), ((), ()))

        def gate_body(i, carry):
            span = pl.ds(pl.multiple_of(i * TILE, TILE), TILE)
            act = lax.dot_general(
                rows[p][:, :half], gate_all[span, near], contract, preferred_element_type=f32
            )
            swap = lax.dot_general(
                rows[p][:, half:], gate_all[span, far], contract, preferred_element_type=f32
            )
            pieces = []
            for s in range(8):
                for real, r0 in ((s, 0), (s ^ 4, size // 2)):
                    a, b = real * size + r0, (real ^ 4) * size + r0
                    pieces.append(act[a : a + size // 2] + swap[b : b + size // 2])
            act = jnp.concatenate(pieces, axis=0)
            hid[pl.ds(0, total), span] = (act / (1.0 + jnp.exp(-act))).astype(bf16)
            for at, hook in gate_hooks:
                pl.when(i == at)(hook)
            return carry

        lax.fori_loop(0, hidden // TILE, gate_body, 0)
        if before_down is not None:
            before_down()

        def down_body(i, carry):
            span = pl.ds(pl.multiple_of(i * TILE, TILE), TILE)
            value = jnp.dot(
                hid[pl.ds(0, total), :], down_all[:, span], preferred_element_type=f32
            )
            partial[p][:, span] = value.astype(bf16)
            for at, hook in down_hooks:
                pl.when(i == at)(hook)
            return carry

        lax.fori_loop(0, width // TILE, down_body, 0)

    def step(fn, *args):
        return lambda: fn(*args)

    def weights_here(k):
        weights[k][0].wait()
        weights[k][1].wait_recv()

    dispatch(0)
    dispatch(1)
    ag(0, 0)
    dispatch(2)
    dispatch(3)
    ag(1, 0)
    ag(0, 1)
    ag(2, 0)
    ag(1, 1)
    ag(0, 2)
    ag(3, 0)
    ag(2, 1)
    ag(1, 2)
    ag(0, 3)
    weights_here(0)
    compute(
        0,
        [(1, step(ag, 3, 1)), (4, step(ag, 2, 2))],
        [(1, step(ag, 3, 2))],
        lambda: weights_here(1),
    )
    rs(0, 0)
    ag(1, 3)
    compute(1, [(1, step(rs, 0, 1)), (5, step(rs, 0, 2))], [(10, step(rs, 0, 3))])
    rs(1, 0)
    ag(2, 3)
    compute(2, [(2, step(rs, 1, 1))], [(0, step(rs, 1, 2)), (12, step(rs, 1, 3))])
    rs(2, 0)
    ag(3, 3)
    compute(3, [(3, step(rs, 2, 1))], [(6, step(rs, 2, 2))])
    rs(3, 0)
    rs(2, 3)
    rs(3, 1)
    rs(3, 2)

    gap = gap_ref[...]
    table = jnp.concatenate(
        [row.astype(f32) for row in code_rows]
        + [1.0 / (1.0 + jnp.exp(-gap)), 1.0 / (1.0 + jnp.exp(gap))]
        + [jnp.zeros((WIN - 6, WIN), f32)],
        axis=0,
    )
    table = jnp.transpose(table)
    place = [table[:, k : k + 1] for k in range(4)]
    weight = [table[:, 4:5], table[:, 5:6]]
    rs(3, 3)
    for copies in returns:
        for copy in copies:
            copy.wait_recv()

    def weighed(length, which, offset):
        at = lax.broadcasted_iota(i32, (WIN, length), 1).astype(f32) - float(offset)
        total = jnp.zeros((WIN, length), f32)
        for k in (0, 1):
            total = total + jnp.where(at == place[2 * k + which], weight[k], 0.0)
        return total.astype(bf16)

    wide, thin = back_a.shape[1], back_b.shape[1]
    for q in range(width // wide):
        mixed = jnp.dot(weighed(384, 0, q), back_a[...], preferred_element_type=f32)
        more = [
            jnp.dot(weighed(128, 1, n), back_b[...], preferred_element_type=f32)
            for n in range(q * wide // thin, (q + 1) * wide // thin)
        ]
        out_ref[:, q * wide : (q + 1) * wide] = (mixed + jnp.concatenate(more, axis=1)).astype(bf16)

    for copy in sent:
        copy.wait_send()


def local(pool, picks, lengths, routes, route_gap, gate_weight, down_weight):
    width = gate_weight.shape[2]
    hidden = 2 * gate_weight.shape[1]
    feats = pool.shape[2]
    bf16 = jnp.bfloat16
    dma = pltpu.SemaphoreType.DMA
    most = max(r for _, r in PARTS)
    scratch = [
        pltpu.VMEM((hidden, width), bf16),
        pltpu.VMEM((hidden, width), bf16),
        pltpu.VMEM((8 * most, hidden), bf16),
        pltpu.VMEM((EXPERTS, 8, WIN), jnp.int32),
        pltpu.VMEM((EXPERTS * WIN, feats), bf16),
        pltpu.VMEM((384, width // 4), bf16),
        pltpu.VMEM((128, width // 8), bf16),
    ]
    for shape in (
        lambda r: (8 * r, width),
        lambda r: (8 * r, width),
        lambda r: (7 * r, width),
        lambda r: (8 * r, feats),
        lambda r: (128, width * r // 128),
        lambda r: (128, width * r // 128),
    ):
        scratch += [pltpu.VMEM(shape(r), bf16) for _, r in PARTS]
    scratch += [dma((9 * COUNT,)) for _ in range(4)] + [dma((2,)) for _ in range(3)]
    scratch += [dma((7,)) for _ in range(2)] + [dma((7 * COUNT,)) for _ in range(4)]
    vmem = pl.BlockSpec(memory_space=pltpu.VMEM)
    smem = pl.BlockSpec(memory_space=pltpu.SMEM)
    hbm = pl.BlockSpec(memory_space=pl.ANY)
    return pl.pallas_call(
        layer_kernel,
        out_shape=jax.ShapeDtypeStruct((WIN, width), bf16),
        in_specs=[smem, smem, vmem, vmem, vmem, hbm, hbm],
        out_specs=vmem,
        scratch_shapes=scratch,
        compiler_params=pltpu.CompilerParams(
            collective_id=0, has_side_effects=True, vmem_limit_bytes=67043328
        ),
        name="layer",
    )(
        picks, lengths, routes.T, route_gap.reshape(1, WIN), pool, gate_weight[0], down_weight[0]
    )


def solution(mesh):
    placed = (
        P("fsdp", None, "expert"),
        P("fsdp", None),
        P("fsdp"),
        P(("fsdp", "expert"), None),
        P(("fsdp", "expert")),
        P("expert", "fsdp", None),
        P("expert", "fsdp", None),
    )
    return jax.shard_map(
        local, mesh=mesh, in_specs=placed, out_specs=P(("fsdp", "expert"), None), check_vma=False
    )
```

time: 202 us -> 161 us (0.80)
  Pallas kernels: 137 us -> 158 us
  blocking collectives: 19.6 us -> 0 us
  waiting for transfers between devices: 13.7 us -> 0 us
  starting transfers between devices: 11.4 us -> 0 us
  local copies, waits for them, and re-layouts: 10.8 us -> 2.29 us
  other arithmetic: 6.22 us -> 0 us
    pallas_call x1, Pallas kernels: 137 us -> 158 us  [local(): pl.pallas_call(layer_kernel, out_shape=jax.ShapeDtypeStruct((WIN, width),...]
    all_to_all x1 -> x0, blocking collectives: 19.6 us -> none  [local(): lax.all_to_all(outgoing, 'expert', split_axis=1, concat_axis=4, tiled=True)]
    all_to_all x2 -> x0, waiting for transfers between devices: 13.7 us -> none  [the longest x1 11 us: local(): lax.all_to_all(expert_out, 'expert', split_axis=0, concat_axis=1, tiled=T...]
    all_to_all x2 -> x0, starting transfers between devices: 11.4 us -> none  [the longest x1 7.89 us: sent_to_all(): lax.all_to_all(jnp.broadcast_to(value[None], (length, *value.shape)), axi...]
    another operation x2 -> x0, other arithmetic: 4.58 us -> none
    gather x2 -> x0, local copies, waits for them, and re-layouts: 3.5 us -> none  [the longest x1 2.21 us: local(): selected = jnp.take(pool, chosen, axis=0)]
    reshape x2 -> x0, local copies, waits for them, and re-layouts: 2.69 us -> none  [the longest x1 2.42 us: local(): expert_out = summed.reshape(expert_count, expert_local, CAP, model_width)]
  transfers between devices with their start and end apart: 2 -> 0, of which waited for: 2 -> 0; matrix products, arithmetic and copies ran while one was open for 3% -> 0% of each run, Pallas kernels for 0% -> 0%
where the time goes in v2:
time: 161 us; the launch traced here: 160 us
  Pallas kernels  158 us (98%)
  local copies, waits for them, and re-layouts  2.29 us (1%)
    pallas_call x1, Pallas kernels, local(): pl.pallas_call(layer_kernel, out_shape=jax.ShapeDtypeStruct((WIN, width),...  158 us

profile of v2, /device:TPU:0, one launch (start us, length us, event | category | flops | bytes accessed | tf_op | source)
XLA Modules:
  0.0 160.1 jit_solution(2703794626076446328)
XLA Ops:
  0.0 157.8 %layer.1 = bf16[128,4096]{1,0:T(8,128)(2,1)} custom-call(s32[1,8]{1,0:T(1,128)} %picks_ref.1, s32[16]{0:T(128)} %lengths_ref.1, s32[2,128]{1,0:T(2,128)} %bitcast.6, f32[1,128]{1,0:T(1,128)} %bitcast.7, bf16[16,128,512]{2,1,0:T(8,128)(2,1)} %pool_ref.1, bf16[896,4096]{1,0:T(8,128)(2,1)} %bitcast.4, bf16[896,4096]{1,0:T(8,128)(2,1)} %bitcast.5), custom_call_target="tpu_custom_call" | custom-call | tf_op jit(solution)/shard_map/layer/pallas_call | solution.py:512
  157.8 2.3 %copy.9 = bf16[128,4096]{1,0:T(8,128)(2,1)} copy(bf16[128,4096]{1,0:T(8,128)(2,1)} %layer.1) | data formatting | bytes 2097152

commit v3 on v2

--- a/solution.py
+++ b/solution.py
@@ -12,22 +12,61 @@
 PARTS = (("A", 32), ("B", 32), ("A", 32), ("B", 16))
 COUNT = len(PARTS)
 STARTS = tuple(sum(r for _, r in PARTS[:p]) for p in range(COUNT))
+SIZES = sorted({r for _, r in PARTS}, reverse=True)
+NTH = tuple(sum(q == r for _, q in PARTS[:p]) for p, (_, r) in enumerate(PARTS))
+MANY = {r: sum(q == r for _, q in PARTS) for r in SIZES}
 TILE = 256
+WIDE = 1024
 CHUNK = 512
 NOWHERE = -4096
+
+ORDER = (
+    (0, "go"), (1, "go"), (2, "go"), (3, "go"), (0, "x0"), (0, "m0"),
+    (0, "p0"), (1, "m0"), (1, "p0"), (1, "x0"), (0, "m1"), (0, "p1"),
+    (2, "x0"), (1, "ph0"), (1, "x3"), (1, "mh0"), (0, "ph0"), (0, "mh0"),
+    (0, "ph1"), (0, "mh1"), (1, "x1"), (2, "m1"), (3, "p0"), (1, "x2"),
+    (2, "p1"),
+    (
+        0,
+        {2: [(3, "m0")], 5: [(3, "x3"), (2, "p0"), (2, "m0")]},
+        {1: [(3, "x0")]},
+    ),
+    (3, "mh0"), (3, "ph0"), (3, "x1"),
+    (
+        1,
+        {1: [(2, "mh1"), (0, "rhp1")], 5: [(2, "ph0"), (2, "mh0")], 6: [(3, "x2")]},
+        {1: [(2, "ph1"), (0, "rhm0")]},
+    ),
+    (1, "rx1"), (0, "rhp0"), (0, "rhm1"), (0, "rfp1"), (0, "rfm0"),
+    (
+        2,
+        {1: [(1, "rx0")], 5: [(0, "rfm1"), (0, "rfp0")]},
+        {0: [(1, "rx2")]},
+    ),
+    (2, "rhm0"), (2, "rhp1"),
+    (
+        3,
+        {1: [(1, "rx3")], 2: [(2, "rhm1"), (2, "rhp0")], 6: [(1, "rhp"), (2, "rfm0")]},
+        {0: [(0, "rx")], 1: [(2, "rfp1")]},
+    ),
+    (2, "rfm1"), (3, "rx2"), (1, "rfp"), (3, "rx3"), (0, "rend"), (1, "rhm"),
+    (3, "rx1"), (3, "rhm"), (3, "rhp"), (2, "rfp0"), (2, "rx"), (1, "rfm"),
+    (3, "rfp"), (3, "rx0"), (3, "rfm"), (2, "rend"), (1, "rend"), (3, "rend"),
+)
 
 
 def layer_kernel(
     picks_ref, lengths_ref, routes_ref, gap_ref, pool_ref, gate_ref, down_ref, out_ref, *rest
 ):
-    gate_all, down_all, hid, keys, tokens, back_a, back_b = rest[:7]
-    rest = rest[7:]
+    gate_all, down_all, hid, keys, pool, tokens = rest[:6]
+    backs = dict(zip(SIZES, rest[6:]))
+    rest = rest[6 + len(SIZES) :]
     rows, partial, land, ready, summed, packed = (
         rest[k * COUNT : (k + 1) * COUNT] for k in range(6)
     )
     (
         ag_send, ag_recv, rs_send, rs_recv, w_send, w_recv, w_local,
-        key_send, key_recv, go_send, go_recv, ret_send, ret_recv,
+        key_send, key_recv, go_send, go_recv, ret_send, ret_recv, pool_sem,
     ) = rest[6 * COUNT :]
     f32, bf16, i32 = jnp.float32, jnp.bfloat16, jnp.int32
     width = out_ref.shape[1]
@@ -68,6 +107,9 @@
     greeted += [crossed(dx, dz) for dx, dz in others if dx]
     for dev in greeted:
         pl.semaphore_signal(barrier, inc=1, device_id=dev, device_id_type=pl.DeviceIdType.MESH)
+
+    pool_copy = pltpu.make_async_copy(pool_ref, pool, pool_sem.at[0])
+    pool_copy.start()
 
     length = lengths_ref[picks_ref[0, col]]
     lane = lax.broadcasted_iota(i32, (EXPERTS, WIN), 1)
@@ -84,18 +126,23 @@
     for k in (0, 1):
         rank = jnp.sum(hits[k] * earlier[k], axis=0, keepdims=True).astype(i32)
         kept = (lane[:1] < length) & (rank < CAP)
-        low = rank < 12
         split = jnp.where(xh == ids[k] // 4, 0, 1)
-        key = jnp.where(
-            low,
-            (rank // 4) * 256 + ids[k] * 32 + split * 16 + z * 4 + rank % 4,
-            768 + ids[k] * 16 + split * 8 + z * 2 + rank - 12,
-        )
-        key_rows.append(jnp.where(kept, key, NOWHERE))
-        code_rows.append(
-            jnp.where(kept & low, (rank // 4) * 128 + ids[k] * 16 + (rank % 4) * 4, NOWHERE)
-        )
-        code_rows.append(jnp.where(kept & (rank >= 12), ids[k] * 16 + (rank - 12) * 8, NOWHERE))
+        key = jnp.full((1, WIN), NOWHERE, i32)
+        codes = {r: key for r in SIZES}
+        for p, (_, size) in enumerate(PARTS):
+            slots, first = size // 8, STARTS[p] // 8
+            here = kept & (rank >= first) & (rank < first + slots)
+            at = rank - first
+            key = jnp.where(
+                here,
+                8 * STARTS[p] + ids[k] * size + split * (size // 2) + z * slots + at,
+                key,
+            )
+            codes[size] = jnp.where(
+                here, NTH[p] * 128 + ids[k] * 16 + at * (128 // size), codes[size]
+            )
+        key_rows.append(key)
+        code_rows.append(codes)
     key_block = jnp.concatenate(
         [key_rows[0], key_rows[1], jnp.full((6, WIN), NOWHERE, i32)], axis=0
     )
@@ -103,7 +150,7 @@
 
     pl.semaphore_wait(barrier, len(greeted))
 
-    sent = []
+    sent, waited = [], set()
 
     def remote(src, dst, send_sem, recv_sem, dev):
         copy = pltpu.make_async_remote_copy(
@@ -114,15 +161,18 @@
             device_id=dev,
             device_id_type=pl.DeviceIdType.MESH,
         )
-        sent.append(copy)
         return copy
 
     key_copies = [
         remote(keys.at[col], keys.at[col], key_send.at[n], key_recv.at[n], same(dx, dz))
         for n, (dx, dz) in enumerate(others)
     ]
+    def begin(copy):
+        sent.append(copy)
+        copy.start()
+
     for copy in key_copies:
-        copy.start()
+        begin(copy)
 
     weights = []
     for k, (src, dst) in enumerate(((gate_ref, gate_all), (down_ref, down_all))):
@@ -131,7 +181,7 @@
             src, dst.at[pl.ds(own_hidden, own_hidden)], w_send.at[k], w_recv.at[k], plane(cn)
         )
         weights.append((kept_half, other))
-        other.start()
+        begin(other)
         kept_half.start()
 
     LEFT, RIGHT, FULL = pl.ds(0, half), pl.ds(half, half), pl.ds(0, width)
@@ -203,7 +253,7 @@
                 for n, (dx, dz) in enumerate(others)
             ]
         )
-        back = back_a.at[pl.ds(p * 128, 128)] if size == 32 else back_b
+        back = backs[size].at[pl.ds(NTH[p] * 128, 128)]
         returns.append(
             [
                 remote(
@@ -215,8 +265,9 @@
             ]
         )
 
+    pool_copy.wait()
     for b in range(EXPERTS):
-        tokens[pl.ds(b * WIN, WIN), :] = pool_ref[picks_ref[0, b]]
+        tokens[pl.ds(b * WIN, WIN), :] = pool[picks_ref[0, b]]
     for copy in key_copies:
         copy.wait_recv()
     all_keys = [
@@ -229,54 +280,31 @@
         table = jnp.where((slot == all_keys[0]) | (slot == all_keys[1]), 1.0, 0.0).astype(bf16)
         ready[p][...] = jnp.dot(table, tokens[...], preferred_element_type=f32).astype(bf16)
         for copy in goes[p]:
-            copy.start()
+            begin(copy)
         rows[p][pl.ds(0, size), pl.ds(pl.multiple_of(z * feats, feats), feats)] = ready[p][
             pl.ds(pl.multiple_of(col * size, size), size), :
         ]
 
-    def steps(copies):
-        def begin(*names):
-            for name in names:
-                copies[name].start()
-
-        def got(*names):
-            for name in names:
-                copies[name].wait_recv()
-
-        return begin, got
-
-    def ag(p, stage):
-        begin, got = steps(gathers[p])
-        if stage == 0:
+    def need(copies, *names):
+        for name in names:
+            copy = copies[name]
+            if id(copy) not in waited:
+                waited.add(id(copy))
+                copy.wait_recv()
+
+    AFTER = {
+        "ph0": ("p0",), "mh0": ("m0",), "p1": ("x0",), "m1": ("x0",), "ph1": ("p1",),
+        "mh1": ("m1",), "x3": ("p0",), "x1": ("m0",), "x2": ("ph0", "mh0"),
+    }
+
+    def gather_step(p, name):
+        if name in AFTER:
+            need(gathers[p], *AFTER[name])
+        elif id(goes[p][0]) not in waited:
             for copy in goes[p]:
+                waited.add(id(copy))
                 copy.wait_recv()
-            begin("p0", "m0", "x0")
-        elif PARTS[p][0] == "A":
-            if stage == 1:
-                got("p0")
-                begin("ph0")
-                got("m0")
-                begin("mh0")
-                got("x0")
-                begin("p1", "m1")
-            elif stage == 2:
-                got("p1")
-                begin("ph1")
-                got("m1")
-                begin("mh1")
-            else:
-                got("ph0", "mh0", "ph1", "mh1")
-        else:
-            if stage == 1:
-                got("p0")
-                begin("ph0", "x3")
-                got("m0")
-                begin("mh0", "x1")
-            elif stage == 2:
-                got("ph0", "mh0")
-                begin("x2")
-            else:
-                got("x0", "x3", "x1", "x2")
+        begin(gathers[p][name])
 
     def add(p, index, terms, last=False):
         size = PARTS[p][1]
@@ -313,59 +341,43 @@
         order = jnp.where((j % per) * size + j // per == i, 1.0, 0.0).astype(bf16)
         packed[p][...] = jnp.dot(order, summed[p][...], preferred_element_type=f32).astype(bf16)
         for copy in returns[p]:
-            copy.start()
+            begin(copy)
         mine = packed[p][pl.ds(pl.multiple_of(z * 16, 16), 16), :]
-        if size == 32:
-            back_a[pl.ds(pl.multiple_of(p * 128 + col * 16, 16), 16), :] = mine
+        backs[size][pl.ds(pl.multiple_of(NTH[p] * 128 + col * 16, 16), 16), :] = mine
+
+    SUM_A = {
+        "fp0": (("hp0",), 1, [(0, LEFT)]), "fp1": (("hp1",), 5, [(1, LEFT)]),
+        "fm0": (("hm0",), 3, [(0, RIGHT)]), "fm1": (("hm1",), 7, [(1, RIGHT)]),
+        "x": (("fp1", "fm1"), 4, [(4, FULL), (5, FULL)]),
+        "end": (("fp0", "fm0", "x"), 0, [(2, FULL), (3, FULL), (6, FULL)]),
+    }
+    SUM_B = {
+        "hp": (("x2",), 2, [(2, LEFT)]), "hm": (("x2",), 2, [(2, RIGHT)]),
+        "fp": (("x1", "hp"), 1, [(1, FULL), (4, LEFT)]),
+        "fm": (("x3", "hm"), 3, [(3, FULL), (4, RIGHT)]),
+        "end": (("x0", "fp", "fm"), 0, [(0, FULL), (5, FULL), (6, FULL)]),
+    }
+
+    def scatter_step(p, name):
+        sums = SUM_A if PARTS[p][0] == "A" else SUM_B
+        if name in sums:
+            names, index, terms = sums[name]
+            need(reduces[p], *names)
+            add(p, index, terms, name == "end")
+        if name == "end":
+            ret(p)
         else:
-            back_b[pl.ds(pl.multiple_of(col * 16, 16), 16), :] = mine
-
-    def rs(p, stage):
-        begin, got = steps(reduces[p])
-        if PARTS[p][0] == "A":
-            if stage == 0:
-                begin("hp0", "hm0", "hp1", "hm1")
-            elif stage == 1:
-                for rx in (1, 0):
-                    got(f"hp{rx}")
-                    add(p, rx * 4 + 1, [(rx, LEFT)])
-                    begin(f"fp{rx}")
-                    got(f"hm{rx}")
-                    add(p, rx * 4 + 3, [(rx, RIGHT)])
-                    begin(f"fm{rx}")
-            elif stage == 2:
-                got("fp1", "fm1")
-                add(p, 4, [(4, FULL), (5, FULL)])
-                begin("x")
-            else:
-                got("fp0", "fm0", "x")
-                add(p, 0, [(2, FULL), (3, FULL), (6, FULL)], True)
-                ret(p)
-        else:
-            if stage == 0:
-                begin("x2", "x1", "x3", "x0")
-            elif stage == 1:
-                got("x2")
-                add(p, 2, [(2, FULL)])
-                begin("hp", "hm")
-            elif stage == 2:
-                got("x1", "hp")
-                add(p, 1, [(1, FULL), (4, LEFT)])
-                begin("fp")
-                got("x3", "hm")
-                add(p, 3, [(3, FULL), (4, RIGHT)])
-                begin("fm")
-            else:
-                got("x0", "fp", "fm")
-                add(p, 0, [(0, FULL), (5, FULL), (6, FULL)], True)
-                ret(p)
-
-    def compute(p, gate_hooks=(), down_hooks=(), before_down=None):
+            begin(reduces[p][name])
+
+    def compute(p, gate_hooks, down_hooks):
         size = PARTS[p][1]
         total = 8 * size
         near = pl.ds(pl.multiple_of(xh * half, half), half)
         far = pl.ds(pl.multiple_of((1 - xh) * half, half), half)
         contract = (((1,), (1,)), ((), ()))
+        need(gathers[p], *gathers[p])
+        if not p:
+            weights_here(0)
 
         def gate_body(i, carry):
             span = pl.ds(pl.multiple_of(i * TILE, TILE), TILE)
@@ -382,98 +394,79 @@
                     pieces.append(act[a : a + size // 2] + swap[b : b + size // 2])
             act = jnp.concatenate(pieces, axis=0)
             hid[pl.ds(0, total), span] = (act / (1.0 + jnp.exp(-act))).astype(bf16)
-            for at, hook in gate_hooks:
-                pl.when(i == at)(hook)
+            for at, hook in gate_hooks.items():
+                pl.when(i == at)(lambda: run(hook))
             return carry
 
         lax.fori_loop(0, hidden // TILE, gate_body, 0)
-        if before_down is not None:
-            before_down()
+        if not p:
+            weights_here(1)
 
         def down_body(i, carry):
-            span = pl.ds(pl.multiple_of(i * TILE, TILE), TILE)
+            span = pl.ds(pl.multiple_of(i * WIDE, WIDE), WIDE)
             value = jnp.dot(
                 hid[pl.ds(0, total), :], down_all[:, span], preferred_element_type=f32
             )
             partial[p][:, span] = value.astype(bf16)
-            for at, hook in down_hooks:
-                pl.when(i == at)(hook)
+            for at, hook in down_hooks.items():
+                pl.when(i == at)(lambda: run(hook))
             return carry
 
-        lax.fori_loop(0, width // TILE, down_body, 0)
-
-    def step(fn, *args):
-        return lambda: fn(*args)
+        lax.fori_loop(0, width // WIDE, down_body, 0)
 
     def weights_here(k):
         weights[k][0].wait()
         weights[k][1].wait_recv()
 
-    dispatch(0)
-    dispatch(1)
-    ag(0, 0)
-    dispatch(2)
-    dispatch(3)
-    ag(1, 0)
-    ag(0, 1)
-    ag(2, 0)
-    ag(1, 1)
-    ag(0, 2)
-    ag(3, 0)
-    ag(2, 1)
-    ag(1, 2)
-    ag(0, 3)
-    weights_here(0)
-    compute(
-        0,
-        [(1, step(ag, 3, 1)), (4, step(ag, 2, 2))],
-        [(1, step(ag, 3, 2))],
-        lambda: weights_here(1),
-    )
-    rs(0, 0)
-    ag(1, 3)
-    compute(1, [(1, step(rs, 0, 1)), (5, step(rs, 0, 2))], [(10, step(rs, 0, 3))])
-    rs(1, 0)
-    ag(2, 3)
-    compute(2, [(2, step(rs, 1, 1))], [(0, step(rs, 1, 2)), (12, step(rs, 1, 3))])
-    rs(2, 0)
-    ag(3, 3)
-    compute(3, [(3, step(rs, 2, 1))], [(6, step(rs, 2, 2))])
-    rs(3, 0)
-    rs(2, 3)
-    rs(3, 1)
-    rs(3, 2)
+    def run(steps):
+        for p, name in steps:
+            if name == "go":
+                dispatch(p)
+            elif name[0] == "r":
+                scatter_step(p, name[1:])
+            else:
+                gather_step(p, name)
+
+    for entry in ORDER:
+        if len(entry) == 3:
+            compute(*entry)
+        else:
+            run((entry,))
 
     gap = gap_ref[...]
+    kinds = len(SIZES)
     table = jnp.concatenate(
-        [row.astype(f32) for row in code_rows]
+        [codes[r].astype(f32) for codes in code_rows for r in SIZES]
         + [1.0 / (1.0 + jnp.exp(-gap)), 1.0 / (1.0 + jnp.exp(gap))]
-        + [jnp.zeros((WIN - 6, WIN), f32)],
+        + [jnp.zeros((WIN - 2 * kinds - 2, WIN), f32)],
         axis=0,
     )
     table = jnp.transpose(table)
-    place = [table[:, k : k + 1] for k in range(4)]
-    weight = [table[:, 4:5], table[:, 5:6]]
-    rs(3, 3)
     for copies in returns:
         for copy in copies:
             copy.wait_recv()
 
-    def weighed(length, which, offset):
+    def weighed(which, offset):
+        length = 128 * MANY[SIZES[which]]
         at = lax.broadcasted_iota(i32, (WIN, length), 1).astype(f32) - float(offset)
         total = jnp.zeros((WIN, length), f32)
         for k in (0, 1):
-            total = total + jnp.where(at == place[2 * k + which], weight[k], 0.0)
+            column_of = k * kinds + which
+            hit = at == table[:, column_of : column_of + 1]
+            total = total + jnp.where(hit, table[:, 2 * kinds + k : 2 * kinds + k + 1], 0.0)
         return total.astype(bf16)
 
-    wide, thin = back_a.shape[1], back_b.shape[1]
-    for q in range(width // wide):
-        mixed = jnp.dot(weighed(384, 0, q), back_a[...], preferred_element_type=f32)
-        more = [
-            jnp.dot(weighed(128, 1, n), back_b[...], preferred_element_type=f32)
-            for n in range(q * wide // thin, (q + 1) * wide // thin)
-        ]
-        out_ref[:, q * wide : (q + 1) * wide] = (mixed + jnp.concatenate(more, axis=1)).astype(bf16)
+    most = backs[SIZES[0]].shape[1]
+    for q in range(width // most):
+        mixed = jnp.zeros((WIN, most), f32)
+        for which, size in enumerate(SIZES):
+            block = backs[size].shape[1]
+            pieces = [
+                jnp.dot(weighed(which, n), backs[size][...], preferred_element_type=f32)
+                for n in range(q * most // block, (q + 1) * most // block)
+            ]
+            mixed = mixed + (pieces[0] if len(pieces) == 1 else jnp.concatenate(pieces, axis=1))
+        out_ref[:, q * most : (q + 1) * most] = mixed.astype(bf16)
 
     for copy in sent:
         copy.wait_send()
@@ -491,10 +484,10 @@
         pltpu.VMEM((hidden, width), bf16),
         pltpu.VMEM((8 * most, hidden), bf16),
         pltpu.VMEM((EXPERTS, 8, WIN), jnp.int32),
+        pltpu.VMEM(pool.shape, bf16),
         pltpu.VMEM((EXPERTS * WIN, feats), bf16),
-        pltpu.VMEM((384, width // 4), bf16),
-        pltpu.VMEM((128, width // 8), bf16),
     ]
+    scratch += [pltpu.VMEM((128 * MANY[r], width * r // 128), bf16) for r in SIZES]
     for shape in (
         lambda r: (8 * r, width),
         lambda r: (8 * r, width),
@@ -506,13 +499,14 @@
         scratch += [pltpu.VMEM(shape(r), bf16) for _, r in PARTS]
     scratch += [dma((9 * COUNT,)) for _ in range(4)] + [dma((2,)) for _ in range(3)]
     scratch += [dma((7,)) for _ in range(2)] + [dma((7 * COUNT,)) for _ in range(4)]
+    scratch += [dma((1,))]
     vmem = pl.BlockSpec(memory_space=pltpu.VMEM)
     smem = pl.BlockSpec(memory_space=pltpu.SMEM)
     hbm = pl.BlockSpec(memory_space=pl.ANY)
     return pl.pallas_call(
         layer_kernel,
         out_shape=jax.ShapeDtypeStruct((WIN, width), bf16),
-        in_specs=[smem, smem, vmem, vmem, vmem, hbm, hbm],
+        in_specs=[smem, smem, vmem, vmem, hbm, hbm, hbm],
         out_specs=vmem,
         scratch_shapes=scratch,
         compiler_params=pltpu.CompilerParams(

time: 161 us -> 126 us (0.78)
  Pallas kernels: 158 us -> 123 us
    pallas_call x1, Pallas kernels: 158 us -> 123 us  [local(): pl.pallas_call(layer_kernel, out_shape=jax.ShapeDtypeStruct((WIN, width),...]
where the time goes in v3:
time: 126 us; the launch traced here: 125 us
  Pallas kernels  123 us (98%)
  local copies, waits for them, and re-layouts  2.29 us (2%)
    pallas_call x1, Pallas kernels, local(): pl.pallas_call(layer_kernel, out_shape=jax.ShapeDtypeStruct((WIN, width),...  123 us

profile of v3, /device:TPU:0, one launch (start us, length us, event | category | flops | bytes accessed | tf_op | source)
XLA Modules:
  0.0 125.4 jit_solution(7537977288854221870)
XLA Ops:
  0.0 123.1 %layer.1 = bf16[128,4096]{1,0:T(8,128)(2,1)} custom-call(s32[1,8]{1,0:T(1,128)} %picks_ref.1, s32[16]{0:T(128)} %lengths_ref.1, s32[2,128]{1,0:T(2,128)} %bitcast.6, f32[1,128]{1,0:T(1,128)} %bitcast.7, bf16[16,128,512]{2,1,0:T(8,128)(2,1)} %pool_ref.1, bf16[896,4096]{1,0:T(8,128)(2,1)} %bitcast.4, bf16[896,4096]{1,0:T(8,128)(2,1)} %bitcast.5), custom_call_target="tpu_custom_call" | custom-call | tf_op jit(solution)/shard_map/layer/pallas_call | solution.py:506
  123.1 2.3 %copy.9 = bf16[128,4096]{1,0:T(8,128)(2,1)} copy(bf16[128,4096]{1,0:T(8,128)(2,1)} %layer.1) | data formatting | bytes 2097152

commit v4 on v3

--- a/solution.py
+++ b/solution.py
@@ -19,6 +19,22 @@
 WIDE = 1024
 CHUNK = 512
 NOWHERE = -4096
+
+AG_TYPES = {
+    "A": (("p0",), ("m0",), ("x0",), ("p1",), ("m1",), ("ph0", "mh0", "ph1", "mh1")),
+    "B": (("p0",), ("m0",), ("ph0", "mh0"), ("x0", "x3", "x1", "x2")),
+}
+RS_TYPES = {
+    "A": (("hp0",), ("hm0",), ("hp1",), ("hm1",), ("fp1", "fm1"), ("fp0", "fm0", "x")),
+    "B": (("x2",), ("x1",), ("hp",), ("x3",), ("hm",), ("x0", "fp", "fm")),
+}
+MOST = 6
+AG_GROUPS = [AG_TYPES[kind] for kind, _ in PARTS]
+RS_GROUPS = [RS_TYPES[kind] for kind, _ in PARTS]
+
+
+def group_of(groups, name):
+    return [n for n, names in enumerate(groups) if name in names][0]
 
 ORDER = (
     (0, "go"), (1, "go"), (2, "go"), (3, "go"), (0, "x0"), (0, "m0"),
@@ -56,9 +72,11 @@
 
 
 def layer_kernel(
-    picks_ref, lengths_ref, routes_ref, gap_ref, pool_ref, gate_ref, down_ref, out_ref, *rest
+    picks_in, lengths_in, routes_in, gap_in, pool_in, gate_ref, down_ref, out_ref, *rest
 ):
-    gate_all, down_all, hid, keys, pool, tokens = rest[:6]
+    small, rest = rest[:5], rest[5:]
+    picks_ref, lengths_ref, routes_ref, gap_ref, pool = small
+    gate_all, down_all, hid, keys, tokens, so_far = rest[:6]
     backs = dict(zip(SIZES, rest[6:]))
     rest = rest[6 + len(SIZES) :]
     rows, partial, land, ready, summed, packed = (
@@ -66,12 +84,12 @@
     )
     (
         ag_send, ag_recv, rs_send, rs_recv, w_send, w_recv, w_local,
-        key_send, key_recv, go_send, go_recv, ret_send, ret_recv, pool_sem,
+        key_sem, go_send, go_recv, ret_send, ret_recv, in_sem,
     ) = rest[6 * COUNT :]
     f32, bf16, i32 = jnp.float32, jnp.bfloat16, jnp.int32
     width = out_ref.shape[1]
     half = width // 2
-    feats = pool_ref.shape[2]
+    feats = pool_in.shape[2]
     own_hidden = gate_ref.shape[0]
     hidden = 2 * own_hidden
 
@@ -108,8 +126,16 @@
     for dev in greeted:
         pl.semaphore_signal(barrier, inc=1, device_id=dev, device_id_type=pl.DeviceIdType.MESH)
 
-    pool_copy = pltpu.make_async_copy(pool_ref, pool, pool_sem.at[0])
-    pool_copy.start()
+    loads = [
+        pltpu.make_async_copy(src, dst, in_sem.at[k])
+        for k, (src, dst) in enumerate(
+            zip((picks_in, lengths_in, routes_in, gap_in, pool_in), small)
+        )
+    ]
+    for copy in loads:
+        copy.start()
+    for copy in loads[:4]:
+        copy.wait()
 
     length = lengths_ref[picks_ref[0, col]]
     lane = lax.broadcasted_iota(i32, (EXPERTS, WIN), 1)
@@ -150,10 +176,10 @@
 
     pl.semaphore_wait(barrier, len(greeted))
 
-    sent, waited = [], set()
+    waited = set()
 
     def remote(src, dst, send_sem, recv_sem, dev):
-        copy = pltpu.make_async_remote_copy(
+        return pltpu.make_async_remote_copy(
             src_ref=src,
             dst_ref=dst,
             send_sem=send_sem,
@@ -161,18 +187,16 @@
             device_id=dev,
             device_id_type=pl.DeviceIdType.MESH,
         )
-        return copy
+
+    def arrivals(like, sem):
+        return remote(like, like, sem, sem, plane(cn))
 
     key_copies = [
-        remote(keys.at[col], keys.at[col], key_send.at[n], key_recv.at[n], same(dx, dz))
-        for n, (dx, dz) in enumerate(others)
+        remote(keys.at[col], keys.at[col], key_sem.at[0], key_sem.at[1], same(dx, dz))
+        for dx, dz in others
     ]
-    def begin(copy):
-        sent.append(copy)
+    for copy in key_copies:
         copy.start()
-
-    for copy in key_copies:
-        begin(copy)
 
     weights = []
     for k, (src, dst) in enumerate(((gate_ref, gate_all), (down_ref, down_all))):
@@ -181,7 +205,7 @@
             src, dst.at[pl.ds(own_hidden, own_hidden)], w_send.at[k], w_recv.at[k], plane(cn)
         )
         weights.append((kept_half, other))
-        begin(other)
+        other.start()
         kept_half.start()
 
     LEFT, RIGHT, FULL = pl.ds(0, half), pl.ds(half, half), pl.ds(0, width)
@@ -194,10 +218,9 @@
             return ref.at[pl.ds(index * size, size), cols]
 
         def gather(name, src, index, cols, dev, p=p, names=names, view=view):
-            n = p * 9 + len(names)
             names[name] = remote(
                 view(rows[p], src, cols), view(rows[p], index, cols),
-                ag_send.at[n], ag_recv.at[n], plane(dev),
+                ag_send.at[p], ag_recv.at[p * MOST + group_of(AG_GROUPS[p], name)], plane(dev),
             )
 
         gather("p0", 0, 3, FULL, yp)
@@ -219,10 +242,9 @@
         sums = {}
 
         def reduce(name, src, index, cols, dev, p=p, sums=sums, view=view):
-            n = p * 9 + len(sums)
             sums[name] = remote(
                 view(partial[p], src, cols), view(land[p], index, cols),
-                rs_send.at[n], rs_recv.at[n], plane(dev),
+                rs_send.at[p], rs_recv.at[p * MOST + group_of(RS_GROUPS[p], name)], plane(dev),
             )
 
         if kind == "A":
@@ -248,9 +270,9 @@
                     rows[p].at[
                         pl.ds(0, size), pl.ds(pl.multiple_of(dx * half + z * feats, feats), feats)
                     ],
-                    go_send.at[p * 7 + n], go_recv.at[p * 7 + n], crossed(dx, dz),
+                    go_send.at[p], go_recv.at[p], crossed(dx, dz),
                 )
-                for n, (dx, dz) in enumerate(others)
+                for dx, dz in others
             ]
         )
         back = backs[size].at[pl.ds(NTH[p] * 128, 128)]
@@ -259,17 +281,16 @@
                 remote(
                     packed[p].at[pl.ds(pl.multiple_of((dx * 4 + (z + dz) % 4) * 16, 16), 16)],
                     back.at[pl.ds(pl.multiple_of(col * 16, 16), 16)],
-                    ret_send.at[p * 7 + n], ret_recv.at[p * 7 + n], crossed(dx, dz),
+                    ret_send.at[p], ret_recv.at[p], crossed(dx, dz),
                 )
-                for n, (dx, dz) in enumerate(others)
+                for dx, dz in others
             ]
         )
 
-    pool_copy.wait()
+    loads[4].wait()
     for b in range(EXPERTS):
         tokens[pl.ds(b * WIN, WIN), :] = pool[picks_ref[0, b]]
-    for copy in key_copies:
-        copy.wait_recv()
+    arrivals(keys.at[pl.ds(0, 7)], key_sem.at[1]).wait_recv()
     all_keys = [
         jnp.concatenate([keys[b, k : k + 1, :] for b in range(EXPERTS)], axis=1) for k in (0, 1)
     ]
@@ -280,17 +301,28 @@
         table = jnp.where((slot == all_keys[0]) | (slot == all_keys[1]), 1.0, 0.0).astype(bf16)
         ready[p][...] = jnp.dot(table, tokens[...], preferred_element_type=f32).astype(bf16)
         for copy in goes[p]:
-            begin(copy)
+            copy.start()
         rows[p][pl.ds(0, size), pl.ds(pl.multiple_of(z * feats, feats), feats)] = ready[p][
             pl.ds(pl.multiple_of(col * size, size), size), :
         ]
 
-    def need(copies, *names):
+    def need(p, ref, sems, groups, *names):
         for name in names:
-            copy = copies[name]
-            if id(copy) not in waited:
-                waited.add(id(copy))
-                copy.wait_recv()
+            n = group_of(groups[p], name)
+            key = (sems is rs_recv, p, n)
+            if key not in waited:
+                waited.add(key)
+                count = sum(2 - ("h" in each) for each in groups[p][n]) * PARTS[p][1]
+                like = ref.at[pl.ds(0, max(count // 2, PARTS[p][1]))]
+                if count == PARTS[p][1]:
+                    like = like.at[:, LEFT]
+                arrivals(like, sems.at[p * MOST + n]).wait_recv()
+
+    def gathered(p, *names):
+        need(p, rows[p], ag_recv, AG_GROUPS, *names)
+
+    def landed(p, *names):
+        need(p, land[p], rs_recv, RS_GROUPS, *names)
 
     AFTER = {
         "ph0": ("p0",), "mh0": ("m0",), "p1": ("x0",), "m1": ("x0",), "ph1": ("p1",),
@@ -299,12 +331,11 @@
 
     def gather_step(p, name):
         if name in AFTER:
-            need(gathers[p], *AFTER[name])
-        elif id(goes[p][0]) not in waited:
-            for copy in goes[p]:
-                waited.add(id(copy))
-                copy.wait_recv()
-        begin(gathers[p][name])
+            gathered(p, *AFTER[name])
+        elif p not in waited:
+            waited.add(p)
+            arrivals(rows[p].at[pl.ds(0, 7 * PARTS[p][1]), pl.ds(0, feats)], go_recv.at[p]).wait_recv()
+        gathers[p][name].start()
 
     def add(p, index, terms, last=False):
         size = PARTS[p][1]
@@ -341,7 +372,7 @@
         order = jnp.where((j % per) * size + j // per == i, 1.0, 0.0).astype(bf16)
         packed[p][...] = jnp.dot(order, summed[p][...], preferred_element_type=f32).astype(bf16)
         for copy in returns[p]:
-            begin(copy)
+            copy.start()
         mine = packed[p][pl.ds(pl.multiple_of(z * 16, 16), 16), :]
         backs[size][pl.ds(pl.multiple_of(NTH[p] * 128 + col * 16, 16), 16), :] = mine
 
@@ -362,12 +393,12 @@
         sums = SUM_A if PARTS[p][0] == "A" else SUM_B
         if name in sums:
             names, index, terms = sums[name]
-            need(reduces[p], *names)
+            landed(p, *names)
             add(p, index, terms, name == "end")
         if name == "end":
             ret(p)
         else:
-            begin(reduces[p][name])
+            reduces[p][name].start()
 
     def compute(p, gate_hooks, down_hooks):
         size = PARTS[p][1]
@@ -375,7 +406,7 @@
         near = pl.ds(pl.multiple_of(xh * half, half), half)
         far = pl.ds(pl.multiple_of((1 - xh) * half, half), half)
         contract = (((1,), (1,)), ((), ()))
-        need(gathers[p], *gathers[p])
+        gathered(p, *gathers[p])
         if not p:
             weights_here(0)
 
@@ -442,34 +473,43 @@
         axis=0,
     )
     table = jnp.transpose(table)
-    for copies in returns:
-        for copy in copies:
-            copy.wait_recv()
-
-    def weighed(which, offset):
-        length = 128 * MANY[SIZES[which]]
-        at = lax.broadcasted_iota(i32, (WIN, length), 1).astype(f32) - float(offset)
-        total = jnp.zeros((WIN, length), f32)
+    def mixed(p, n):
+        size = PARTS[p][1]
+        at = lax.broadcasted_iota(i32, (WIN, 128), 1).astype(f32) + float(NTH[p] * 128 - n)
+        total = jnp.zeros((WIN, 128), f32)
         for k in (0, 1):
-            column_of = k * kinds + which
-            hit = at == table[:, column_of : column_of + 1]
+            which = k * kinds + SIZES.index(size)
+            hit = at == table[:, which : which + 1]
             total = total + jnp.where(hit, table[:, 2 * kinds + k : 2 * kinds + k + 1], 0.0)
-        return total.astype(bf16)
-
-    most = backs[SIZES[0]].shape[1]
-    for q in range(width // most):
-        mixed = jnp.zeros((WIN, most), f32)
-        for which, size in enumerate(SIZES):
-            block = backs[size].shape[1]
-            pieces = [
-                jnp.dot(weighed(which, n), backs[size][...], preferred_element_type=f32)
-                for n in range(q * most // block, (q + 1) * most // block)
-            ]
-            mixed = mixed + (pieces[0] if len(pieces) == 1 else jnp.concatenate(pieces, axis=1))
-        out_ref[:, q * most : (q + 1) * most] = mixed.astype(bf16)
-
-    for copy in sent:
-        copy.wait_send()
+        return jnp.dot(
+            total.astype(bf16), backs[size][pl.ds(NTH[p] * 128, 128), :], preferred_element_type=f32
+        )
+
+    flat = [e for entry in ORDER for e in (entry if len(entry) == 3 else (entry,))]
+    flat = [e for f in flat for e in (sum(f.values(), []) if isinstance(f, dict) else (f,))]
+    ends = [e[0] for e in flat if isinstance(e, tuple) and e[1] == "rend"]
+    for p in ends:
+        size = PARTS[p][1]
+        arrivals(packed[p].at[pl.ds(0, 112)], ret_recv.at[p]).wait_recv()
+        block = backs[PARTS[p][1]].shape[1]
+        for n in range(width // block):
+            cols = pl.ds(n * block, block)
+            total = mixed(p, n)
+            if p != ends[0]:
+                total = total + so_far[:, cols]
+            if p != ends[-1]:
+                so_far[:, cols] = total
+            else:
+                out_ref[:, cols] = total.astype(bf16)
+
+    arrivals(keys.at[pl.ds(0, 7)], key_sem.at[0]).wait_send()
+    for _, other in weights:
+        other.wait_send()
+    for p, (_, size) in enumerate(PARTS):
+        arrivals(land[p], ag_send.at[p]).wait_send()
+        arrivals(land[p], rs_send.at[p]).wait_send()
+        arrivals(rows[p].at[pl.ds(0, 7 * size), pl.ds(0, feats)], go_send.at[p]).wait_send()
+        arrivals(packed[p].at[pl.ds(0, 112)], ret_send.at[p]).wait_send()
 
 
 def local(pool, picks, lengths, routes, route_gap, gate_weight, down_weight):
@@ -480,12 +520,17 @@
     dma = pltpu.SemaphoreType.DMA
     most = max(r for _, r in PARTS)
     scratch = [
+        pltpu.SMEM(picks.shape, jnp.int32),
+        pltpu.SMEM(lengths.shape, jnp.int32),
+        pltpu.VMEM((2, WIN), jnp.int32),
+        pltpu.VMEM((1, WIN), jnp.float32),
+        pltpu.VMEM(pool.shape, bf16),
         pltpu.VMEM((hidden, width), bf16),
         pltpu.VMEM((hidden, width), bf16),
         pltpu.VMEM((8 * most, hidden), bf16),
         pltpu.VMEM((EXPERTS, 8, WIN), jnp.int32),
-        pltpu.VMEM(pool.shape, bf16),
         pltpu.VMEM((EXPERTS * WIN, feats), bf16),
+        pltpu.VMEM((WIN, width), jnp.float32),
     ]
     scratch += [pltpu.VMEM((128 * MANY[r], width * r // 128), bf16) for r in SIZES]
     for shape in (
@@ -497,20 +542,16 @@
         lambda r: (128, width * r // 128),
     ):
         scratch += [pltpu.VMEM(shape(r), bf16) for _, r in PARTS]
-    scratch += [dma((9 * COUNT,)) for _ in range(4)] + [dma((2,)) for _ in range(3)]
-    scratch += [dma((7,)) for _ in range(2)] + [dma((7 * COUNT,)) for _ in range(4)]
-    scratch += [dma((1,))]
-    vmem = pl.BlockSpec(memory_space=pltpu.VMEM)
-    smem = pl.BlockSpec(memory_space=pltpu.SMEM)
-    hbm = pl.BlockSpec(memory_space=pl.ANY)
+    scratch += [dma((COUNT,)), dma((MOST * COUNT,)), dma((COUNT,)), dma((MOST * COUNT,))]
+    scratch += [dma((2,)) for _ in range(4)] + [dma((COUNT,)) for _ in range(4)] + [dma((5,))]
     return pl.pallas_call(
         layer_kernel,
-        out_shape=jax.ShapeDtypeStruct((WIN, width), bf16),
-        in_specs=[smem, smem, vmem, vmem, hbm, hbm, hbm],
-        out_specs=vmem,
+        out_shape=pltpu.VMEM((WIN, width), bf16),
+        in_specs=[pl.BlockSpec(memory_space=pl.ANY)] * 7,
+        out_specs=pl.BlockSpec(memory_space=pltpu.VMEM),
         scratch_shapes=scratch,
         compiler_params=pltpu.CompilerParams(
-            collective_id=0, has_side_effects=True, vmem_limit_bytes=67043328
+            collective_id=0, has_side_effects=True, vmem_limit_bytes=65200000
         ),
         name="layer",
     )(

time: 126 us -> 120 us (0.952)
  Pallas kernels: 123 us -> 119 us
  local copies, waits for them, and re-layouts: 2.29 us -> 0.97 us
    pallas_call x1, Pallas kernels: 123 us -> 119 us  [local(): pl.pallas_call(layer_kernel, out_shape=pltpu.VMEM((WIN, width), bf16), in...]
    unnamed x1, local copies, waits for them, and re-layouts: 2.29 us -> 0.97 us
where the time goes in v4:
time: 120 us
  Pallas kernels  119 us (99%)
    pallas_call x1, Pallas kernels, local(): pl.pallas_call(layer_kernel, out_shape=pltpu.VMEM((WIN, width), bf16), in...  119 us

profile of v4, /device:TPU:0, one launch (start us, length us, event | category | flops | bytes accessed | tf_op | source)
XLA Modules:
  0.0 119.6 jit_solution(12683381945648093075)
XLA Ops:
  0.0 118.6 %layer.1 = bf16[128,4096]{1,0:T(8,128)(2,1)S(1)} custom-call(s32[1,8]{1,0:T(1,128)} %picks_in.1, s32[16]{0:T(128)} %lengths_in.1, s32[2,128]{1,0:T(2,128)} %bitcast.6, f32[1,128]{1,0:T(1,128)} %bitcast.7, bf16[16,128,512]{2,1,0:T(8,128)(2,1)} %pool_in.1, bf16[896,4096]{1,0:T(8,128)(2,1)} %bitcast.4, bf16[896,4096]{1,0:T(8,128)(2,1)} %bitcast.5), custom_call_target="tpu_custom_call" | custom-call | tf_op jit(solution)/shard_map/layer/pallas_call | solution.py:547
  118.6 1.0 copy.9

commit v5 on v4

--- a/solution.py
+++ b/solution.py
@@ -35,6 +35,12 @@
 
 def group_of(groups, name):
     return [n for n, names in enumerate(groups) if name in names][0]
+
+EARLY = (0, 1)
+FRONT = (
+    (0, -2), (0, -1), (1, -2), (1, -1), (0, 0), (0, 1), (2, -2), (1, 0), (1, 1),
+    (0, 2), (3, -2), (0, 3), (1, 2), (1, 3),
+) + tuple((p, -2) for p in range(4, COUNT))
 
 ORDER = (
     (0, "go"), (1, "go"), (2, "go"), (3, "go"), (0, "x0"), (0, "m0"),
@@ -108,7 +114,7 @@
     def column(dx, dz):
         return (xh if dx == 0 else 1 - xh) * 4 + (z + dz) % 4
 
-    others = [(dx, dz) for dz in (2, 1, 3, 0) for dx in (1, 0) if dx or dz]
+    others = [(0, 1), (0, 3), (0, 2), (1, 0), (1, 2), (1, 1), (1, 3)]
 
     def plane(dev):
         return {"fsdp": dev, "expert": col}
@@ -169,10 +175,7 @@
             )
         key_rows.append(key)
         code_rows.append(codes)
-    key_block = jnp.concatenate(
-        [key_rows[0], key_rows[1], jnp.full((6, WIN), NOWHERE, i32)], axis=0
-    )
-    keys[col] = key_block
+    keys[col] = jnp.concatenate(key_rows, axis=0)
 
     pl.semaphore_wait(barrier, len(greeted))
 
@@ -270,9 +273,9 @@
                     rows[p].at[
                         pl.ds(0, size), pl.ds(pl.multiple_of(dx * half + z * feats, feats), feats)
                     ],
-                    go_send.at[p], go_recv.at[p], crossed(dx, dz),
+                    go_send.at[p], go_recv.at[p * 4 + min(n, 3)], crossed(dx, dz),
                 )
-                for dx, dz in others
+                for n, (dx, dz) in enumerate(others)
             ]
         )
         back = backs[size].at[pl.ds(NTH[p] * 128, 128)]
@@ -300,11 +303,27 @@
         slot = lax.broadcasted_iota(i32, (8 * size, EXPERTS * WIN), 0) + 8 * STARTS[p]
         table = jnp.where((slot == all_keys[0]) | (slot == all_keys[1]), 1.0, 0.0).astype(bf16)
         ready[p][...] = jnp.dot(table, tokens[...], preferred_element_type=f32).astype(bf16)
-        for copy in goes[p]:
-            copy.start()
         rows[p][pl.ds(0, size), pl.ds(pl.multiple_of(z * feats, feats), feats)] = ready[p][
             pl.ds(pl.multiple_of(col * size, size), size), :
         ]
+        for copy in goes[p]:
+            copy.start()
+
+    def went(p, n):
+        like = rows[p].at[pl.ds(0, PARTS[p][1]), pl.ds(0, feats if n < 3 else half)]
+        arrivals(like, go_recv.at[p * 4 + n]).wait_recv()
+
+    def spread(p, cols):
+        size = PARTS[p][1]
+        for name, index, dev in (("p0", 3, yp), ("m0", 1, ym), ("x0", 4, xn)):
+            remote(
+                rows[p].at[pl.ds(0, size), cols],
+                rows[p].at[pl.ds(index * size, size), cols],
+                ag_send.at[p], ag_recv.at[p * MOST + group_of(AG_GROUPS[p], name)], plane(dev),
+            ).start()
+
+    def slice_of(dz):
+        return pl.ds(pl.multiple_of((z + dz) % 4 * feats, feats), feats)
 
     def need(p, ref, sems, groups, *names):
         for name in names:
@@ -334,7 +353,8 @@
             gathered(p, *AFTER[name])
         elif p not in waited:
             waited.add(p)
-            arrivals(rows[p].at[pl.ds(0, 7 * PARTS[p][1]), pl.ds(0, feats)], go_recv.at[p]).wait_recv()
+            for n in range(4):
+                went(p, n)
         gathers[p][name].start()
 
     def add(p, index, terms, last=False):
@@ -451,12 +471,22 @@
 
     def run(steps):
         for p, name in steps:
-            if name == "go":
-                dispatch(p)
-            elif name[0] == "r":
+            if name == "go" or (p in EARLY and name in ("p0", "m0", "x0")):
+                continue
+            if name[0] == "r":
                 scatter_step(p, name[1:])
             else:
                 gather_step(p, name)
+
+    for step in FRONT:
+        p, n = step
+        if n == -2:
+            dispatch(p)
+        elif n == -1:
+            spread(p, slice_of(0))
+        else:
+            went(p, n)
+            spread(p, RIGHT if n == 3 else slice_of((3, 1, 2)[n]))
 
     for entry in ORDER:
         if len(entry) == 3:
@@ -528,7 +558,7 @@
         pltpu.VMEM((hidden, width), bf16),
         pltpu.VMEM((hidden, width), bf16),
         pltpu.VMEM((8 * most, hidden), bf16),
-        pltpu.VMEM((EXPERTS, 8, WIN), jnp.int32),
+        pltpu.VMEM((EXPERTS, 2, WIN), jnp.int32),
         pltpu.VMEM((EXPERTS * WIN, feats), bf16),
         pltpu.VMEM((WIN, width), jnp.float32),
     ]
@@ -543,7 +573,8 @@
     ):
         scratch += [pltpu.VMEM(shape(r), bf16) for _, r in PARTS]
     scratch += [dma((COUNT,)), dma((MOST * COUNT,)), dma((COUNT,)), dma((MOST * COUNT,))]
-    scratch += [dma((2,)) for _ in range(4)] + [dma((COUNT,)) for _ in range(4)] + [dma((5,))]
+    scratch += [dma((2,)) for _ in range(4)] + [dma((COUNT,)), dma((4 * COUNT,))]
+    scratch += [dma((COUNT,)), dma((COUNT,)), dma((5,))]
     return pl.pallas_call(
         layer_kernel,
         out_shape=pltpu.VMEM((WIN, width), bf16),

time: 120 us -> 118 us (0.983)
  Pallas kernels: 119 us -> 116 us
    pallas_call x1, Pallas kernels: 119 us -> 116 us  [local(): pl.pallas_call(layer_kernel, out_shape=pltpu.VMEM((WIN, width), bf16), in...]
where the time goes in v5:
time: 118 us; the launch traced here: 117 us
  Pallas kernels  116 us (98%)
    pallas_call x1, Pallas kernels, local(): pl.pallas_call(layer_kernel, out_shape=pltpu.VMEM((WIN, width), bf16), in...  116 us

profile of v5, /device:TPU:0, one launch (start us, length us, event | category | flops | bytes accessed | tf_op | source)
XLA Modules:
  0.0 117.4 jit_solution(2189161214293976601)
XLA Ops:
  0.0 116.5 %layer.1 = bf16[128,4096]{1,0:T(8,128)(2,1)S(1)} custom-call(s32[1,8]{1,0:T(1,128)} %picks_in.1, s32[16]{0:T(128)} %lengths_in.1, s32[2,128]{1,0:T(2,128)} %bitcast.6, f32[1,128]{1,0:T(1,128)} %bitcast.7, bf16[16,128,512]{2,1,0:T(8,128)(2,1)} %pool_in.1, bf16[896,4096]{1,0:T(8,128)(2,1)} %bitcast.4, bf16[896,4096]{1,0:T(8,128)(2,1)} %bitcast.5), custom_call_target="tpu_custom_call" | custom-call | tf_op jit(solution)/shard_map/layer/pallas_call | solution.py:578
  116.5 1.0 copy.9

commit v6 on v5

--- a/solution.py
+++ b/solution.py
@@ -9,7 +9,7 @@
 CAP = 14
 WIN = 128
 
-PARTS = (("A", 32), ("B", 32), ("A", 32), ("B", 16))
+PARTS = (("A", 16), ("B", 32), ("A", 32), ("B", 16), ("A", 16))
 COUNT = len(PARTS)
 STARTS = tuple(sum(r for _, r in PARTS[:p]) for p in range(COUNT))
 SIZES = sorted({r for _, r in PARTS}, reverse=True)
@@ -43,37 +43,48 @@
 ) + tuple((p, -2) for p in range(4, COUNT))
 
 ORDER = (
-    (0, "go"), (1, "go"), (2, "go"), (3, "go"), (0, "x0"), (0, "m0"),
-    (0, "p0"), (1, "m0"), (1, "p0"), (1, "x0"), (0, "m1"), (0, "p1"),
-    (2, "x0"), (1, "ph0"), (1, "x3"), (1, "mh0"), (0, "ph0"), (0, "mh0"),
-    (0, "ph1"), (0, "mh1"), (1, "x1"), (2, "m1"), (3, "p0"), (1, "x2"),
-    (2, "p1"),
+    (0, "p1"), (0, "m1"), (2, "x0"), (0, "ph0"), (0, "mh0"), (3, "p0"),
+    (3, "m0"), (1, "x1"), (1, "mh0"), (1, "ph0"), (0, "ph1"), (0, "mh1"),
+    (2, "p1"), (2, "m1"), (1, "x3"),
     (
         0,
-        {2: [(3, "m0")], 5: [(3, "x3"), (2, "p0"), (2, "m0")]},
-        {1: [(3, "x0")]},
+        {0: [(3, "mh0"), (1, "x2"), (3, "ph0")], 2: [(2, "m0"), (2, "p0")]},
+        {0: [(3, "x0")], 1: [(2, "ph1"), (2, "mh1")]},
     ),
-    (3, "mh0"), (3, "ph0"), (3, "x1"),
+    (3, "x2"), (0, "rhp0"), (0, "rhm0"),
     (
         1,
-        {1: [(2, "mh1"), (0, "rhp1")], 5: [(2, "ph0"), (2, "mh0")], 6: [(3, "x2")]},
-        {1: [(2, "ph1"), (0, "rhm0")]},
+        {0: [(0, "rhp1"), (4, "x0"), (4, "m0")],
+         2: [(2, "ph0")],
+         3: [(2, "mh0")],
+         4: [(3, "x3")],
+         5: [(4, "p0")]},
+        {0: [(0, "rhm1"), (3, "x1")], 1: [(0, "rfp1"), (0, "rfm0")]},
     ),
-    (1, "rx1"), (0, "rhp0"), (0, "rhm1"), (0, "rfp1"), (0, "rfm0"),
+    (4, "p1"), (4, "m1"), (1, "rx2"),
     (
         2,
-        {1: [(1, "rx0")], 5: [(0, "rfm1"), (0, "rfp0")]},
-        {0: [(1, "rx2")]},
+        {2: [(4, "mh0"), (4, "ph0")], 4: [(0, "rfm1"), (1, "rx3"), (0, "rfp0")]},
+        {0: [(4, "ph1"), (4, "mh1")], 2: [(1, "rhp"), (1, "rhm"), (1, "rx1")]},
     ),
-    (2, "rhm0"), (2, "rhp1"),
+    (2, "rhp0"), (2, "rhm1"),
     (
         3,
-        {1: [(1, "rx3")], 2: [(2, "rhm1"), (2, "rhp0")], 6: [(1, "rhp"), (2, "rfm0")]},
-        {0: [(0, "rx")], 1: [(2, "rfp1")]},
+        {2: [(2, "rhp1"), (2, "rhm0")], 4: [(0, "rx")], 5: [(1, "rfm")]},
+        {0: [(2, "rfp0"), (1, "rx0")]},
     ),
-    (2, "rfm1"), (3, "rx2"), (1, "rfp"), (3, "rx3"), (0, "rend"), (1, "rhm"),
-    (3, "rx1"), (3, "rhm"), (3, "rhp"), (2, "rfp0"), (2, "rx"), (1, "rfm"),
-    (3, "rfp"), (3, "rx0"), (3, "rfm"), (2, "rend"), (1, "rend"), (3, "rend"),
+    (
+        4,
+        {0: [(1, "rfp"), (2, "rfm0")],
+         1: [(3, "rx1"), (0, "rend")],
+         4: [(3, "rx2")],
+         6: [(2, "rfm1"), (2, "rfp1")]},
+        {0: [(3, "rx0")]},
+    ),
+    (3, "rx3"), (1, "rend"), (4, "rhm1"), (4, "rhp1"), (3, "rhm"), (3, "rhp"),
+    (4, "rhm0"), (4, "rhp0"), (2, "rx"), (4, "rfm1"), (4, "rfp1"), (3, "rfm"),
+    (3, "rfp"), (4, "rfm0"), (4, "rfp0"), (4, "rx"), (2, "rend"), (3, "rend"),
+    (4, "rend"),
 )
 
 
@@ -382,7 +393,7 @@
                     partial[p][pl.ds(index * size, size), cols] = total
                 return carry
 
-            lax.fori_loop(0, half // CHUNK, body, 0)
+            lax.fori_loop(0, half // CHUNK, body, 0, unroll=True)
 
     def ret(p):
         size = PARTS[p][1]

time: 118 us -> 117 us (level)
  no operation moved by 1% of the time
where the time goes in v6:
time: 117 us
  Pallas kernels  116 us (99%)
    pallas_call x1, Pallas kernels, local(): pl.pallas_call(layer_kernel, out_shape=pltpu.VMEM((WIN, width), bf16), in...  116 us

profile of v6, /device:TPU:0, one launch (start us, length us, event | category | flops | bytes accessed | tf_op | source)
XLA Modules:
  0.0 117.2 jit_solution(11373515373505224369)
XLA Ops:
  0.0 116.2 %layer.1 = bf16[128,4096]{1,0:T(8,128)(2,1)S(1)} custom-call(s32[1,8]{1,0:T(1,128)} %picks_in.1, s32[16]{0:T(128)} %lengths_in.1, s32[2,128]{1,0:T(2,128)} %bitcast.6, f32[1,128]{1,0:T(1,128)} %bitcast.7, bf16[16,128,512]{2,1,0:T(8,128)(2,1)} %pool_in.1, bf16[896,4096]{1,0:T(8,128)(2,1)} %bitcast.4, bf16[896,4096]{1,0:T(8,128)(2,1)} %bitcast.5), custom_call_target="tpu_custom_call" | custom-call | tf_op jit(solution)/shard_map/layer/pallas_call | solution.py:589
  116.2 1.0 copy.9

commit v7 on v6

--- a/solution.py
+++ b/solution.py
@@ -514,7 +514,7 @@
         axis=0,
     )
     table = jnp.transpose(table)
-    def mixed(p, n):
+    def shares(p, n):
         size = PARTS[p][1]
         at = lax.broadcasted_iota(i32, (WIN, 128), 1).astype(f32) + float(NTH[p] * 128 - n)
         total = jnp.zeros((WIN, 128), f32)
@@ -522,20 +522,22 @@
             which = k * kinds + SIZES.index(size)
             hit = at == table[:, which : which + 1]
             total = total + jnp.where(hit, table[:, 2 * kinds + k : 2 * kinds + k + 1], 0.0)
-        return jnp.dot(
-            total.astype(bf16), backs[size][pl.ds(NTH[p] * 128, 128), :], preferred_element_type=f32
-        )
+        return total.astype(bf16)
 
     flat = [e for entry in ORDER for e in (entry if len(entry) == 3 else (entry,))]
     flat = [e for f in flat for e in (sum(f.values(), []) if isinstance(f, dict) else (f,))]
     ends = [e[0] for e in flat if isinstance(e, tuple) and e[1] == "rend"]
     for p in ends:
         size = PARTS[p][1]
+        count = width // backs[size].shape[1]
+        share = [shares(p, n) for n in range(count)]
         arrivals(packed[p].at[pl.ds(0, 112)], ret_recv.at[p]).wait_recv()
         block = backs[PARTS[p][1]].shape[1]
         for n in range(width // block):
             cols = pl.ds(n * block, block)
-            total = mixed(p, n)
+            total = jnp.dot(
+                share[n], backs[size][pl.ds(NTH[p] * 128, 128), :], preferred_element_type=f32
+            )
             if p != ends[0]:
                 total = total + so_far[:, cols]
             if p != ends[-1]:

time: 117 us -> 117 us (level)
  no operation moved by 1% of the time
where the time goes in v7:
time: 117 us
  Pallas kernels  116 us (99%)
    pallas_call x1, Pallas kernels, local(): pl.pallas_call(layer_kernel, out_shape=pltpu.VMEM((WIN, width), bf16), in...  116 us

profile of v7, /device:TPU:0, one launch (start us, length us, event | category | flops | bytes accessed | tf_op | source)
XLA Modules:
  0.0 117.2 jit_solution(10592601451241593496)
XLA Ops:
  0.0 116.2 %layer.1 = bf16[128,4096]{1,0:T(8,128)(2,1)S(1)} custom-call(s32[1,8]{1,0:T(1,128)} %picks_in.1, s32[16]{0:T(128)} %lengths_in.1, s32[2,128]{1,0:T(2,128)} %bitcast.6, f32[1,128]{1,0:T(1,128)} %bitcast.7, bf16[16,128,512]{2,1,0:T(8,128)(2,1)} %pool_in.1, bf16[896,4096]{1,0:T(8,128)(2,1)} %bitcast.4, bf16[896,4096]{1,0:T(8,128)(2,1)} %bitcast.5), custom_call_target="tpu_custom_call" | custom-call | tf_op jit(solution)/shard_map/layer/pallas_call | solution.py:591
  116.2 1.0 copy.9
